TPU v7x, 32 devices: a 4x4x1 block of a 4x4x8 slice. The times are simulated.
32 devices in a mesh: dp: 1 (over z), ch: 4 (over y), wd: 8 (over x, core).
Axes of the slice: x: 4, y: 4, z: 1, core: 2. Of those that a mesh axis runs over, the one named last changes fastest.
The devices are a block of a 4x4x8 slice.
Arguments:
- resid_in: bfloat16 [4096, 3072], P('dp', 'wd')
- seg_pos: int32 [1, 4096], P('dp')
- gain_temporal: bfloat16 [3072], P('wd')
- w_x: bfloat16 [3072, 4096], P('wd', 'ch')
- bias_x: bfloat16 [4096], P('ch')
- w_y: bfloat16 [3072, 4096], P('wd', 'ch')
- bias_y: bfloat16 [4096], P('ch')
- conv_w: bfloat16 [4, 4096], P(None, 'ch')
- conv_bias: bfloat16 [4096], P('ch')
- lam_param: float32 [4096], P('ch')
- rgate_w: bfloat16 [16, 256, 256], P('ch')
- rgate_b: bfloat16 [4096], P('ch')
- igate_w: bfloat16 [16, 256, 256], P('ch')
- igate_b: bfloat16 [4096], P('ch')
- w_o: bfloat16 [4096, 3072], P('ch', 'wd')
- bias_o: bfloat16 [3072], P('wd')
- gain_mlp: bfloat16 [3072], P('wd')
- w_g: bfloat16 [3072, 9216], P('wd', 'ch')
- bias_g: bfloat16 [9216], P('ch')
- w_u: bfloat16 [3072, 9216], P('wd', 'ch')
- bias_u: bfloat16 [9216], P('ch')
- w_d: bfloat16 [9216, 3072], P('ch', 'wd')
- bias_d: bfloat16 [3072], P('wd')
Outputs:
- output: bfloat16 [4096, 3072], P('dp', 'wd')
All inputs are finite; a program needn't handle non-finite values.
Results may differ from a plain program's by a relative error of at most 0.0128775.
Values are sent between devices in bfloat16 or wider.
A program may use at most 768 MiB of HBM per device.

v0:
```python
import jax
import jax.numpy as jnp
from jax import lax
from jax.sharding import PartitionSpec as P, NamedSharding

EPS = 1e-6


def rms_apply(vals, sum_sq, width, gain):
    return (vals * lax.rsqrt(sum_sq / width + EPS) * (1.0 + gain.astype(jnp.float32))).astype(jnp.bfloat16)


def token_sum(part_sum, axis_name, count):
    tokens, width = part_sum.shape
    pieces = part_sum.astype(jnp.bfloat16).reshape(count, tokens // count, width)
    received = lax.all_to_all(pieces, axis_name, 0, 0)
    return jnp.sum(received.astype(jnp.float32), axis=0)


def conv_mix(vals, positions, conv_w, conv_bias):
    vals32 = vals.astype(jnp.float32)
    taps = conv_w.astype(jnp.float32)
    total = conv_bias.astype(jnp.float32) + vals32 * taps[0]
    for shift in range(1, conv_w.shape[0]):
        moved = jnp.pad(vals32[:-shift], ((shift, 0), (0, 0)))
        total = total + jnp.where((positions >= shift)[:, None], moved, 0.0) * taps[shift]
    return total.astype(jnp.bfloat16)


def combine(left, right):
    return left[0] * right[0], right[0] * left[1] + right[1]


def rg_lru(conv_out, positions, seqs, lam_param, rgate_w, rgate_b, igate_w, igate_b):
    tokens, width = conv_out.shape
    blocks = rgate_w.shape[0]
    grouped = conv_out.reshape(tokens, blocks, width // blocks)
    rate = jax.nn.sigmoid(jnp.einsum('nbi,bij->nbj', grouped, rgate_w, preferred_element_type=jnp.float32).reshape(tokens, width) + rgate_b.astype(jnp.float32))
    inflow = jax.nn.sigmoid(jnp.einsum('nbi,bij->nbj', grouped, igate_w, preferred_element_type=jnp.float32).reshape(tokens, width) + igate_b.astype(jnp.float32))
    log_a = -8.0 * rate * jax.nn.softplus(-lam_param)
    reset = (positions == 0)[:, None]
    decay = jnp.where(reset, 0.0, jnp.exp(log_a))
    scale = jnp.where(reset, 1.0, jnp.sqrt(-jnp.expm1(2.0 * log_a)))
    drive = scale * inflow * conv_out.astype(jnp.float32)
    steps = tokens // seqs
    hidden = lax.associative_scan(combine, (decay.reshape(seqs, steps, width), drive.reshape(seqs, steps, width)), axis=1)[1]
    return hidden.reshape(tokens, width)


def solution(mesh):
    wd_count = mesh.shape['wd']
    ch_count = mesh.shape['ch']
    row_spec = P('dp', 'wd')
    specs = (row_spec, P('dp', None), P('wd'), P('wd', 'ch'), P('ch'), P('wd', 'ch'), P('ch'), P(None, 'ch'), P('ch'), P('ch'), P('ch', None, None), P('ch'), P('ch', None, None), P('ch'), P('ch', 'wd'), P('wd'), P('wd'), P('wd', 'ch'), P('ch'), P('wd', 'ch'), P('ch'), P('ch', 'wd'), P('wd'))

    def local_layer(resid_in, seg_pos, gain_temporal, w_x, bias_x, w_y, bias_y, conv_w, conv_bias, lam_param, rgate_w, rgate_b, igate_w, igate_b, w_o, bias_o, gain_mlp, w_g, bias_g, w_u, bias_u, w_d, bias_d):
        tokens, local_width = resid_in.shape
        model_width = local_width * wd_count
        share = tokens // ch_count
        positions = seg_pos.reshape(tokens)
        resid32 = resid_in.astype(jnp.float32)
        sum_sq = lax.psum(jnp.sum(resid32 * resid32, axis=1, keepdims=True), 'wd')
        normed = rms_apply(resid32, sum_sq, model_width, gain_temporal)
        y_sum = token_sum(jnp.dot(normed, w_y, preferred_element_type=jnp.float32), 'wd', wd_count)
        y_rows = jax.nn.gelu(y_sum + bias_y.astype(jnp.float32), approximate=True).astype(jnp.bfloat16)
        y_branch = lax.all_gather(y_rows, 'wd', axis=0, tiled=True)
        u_sum = token_sum(jnp.dot(normed, w_x, preferred_element_type=jnp.float32), 'wd', wd_count)
        u_rows = (u_sum + bias_x.astype(jnp.float32)).astype(jnp.bfloat16)
        u_branch = lax.all_gather(u_rows, 'wd', axis=0, tiled=True)
        conv_out = conv_mix(u_branch, positions, conv_w, conv_bias)
        hidden = rg_lru(conv_out, positions, seg_pos.shape[0], lam_param, rgate_w, rgate_b, igate_w, igate_b)
        mixed = (hidden * y_branch.astype(jnp.float32)).astype(jnp.bfloat16)
        mix_sum = token_sum(jnp.dot(mixed, w_o, preferred_element_type=jnp.float32), 'ch', ch_count)
        resid_rows = lax.dynamic_slice_in_dim(resid32, lax.axis_index('ch') * share, share, axis=0)
        resid = resid_rows + mix_sum + bias_o.astype(jnp.float32)
        sum_sq2 = lax.psum(jnp.sum(resid * resid, axis=1, keepdims=True), 'wd')
        normed2 = lax.all_gather(rms_apply(resid, sum_sq2, model_width, gain_mlp), 'ch', axis=0, tiled=True)
        gate_sum = token_sum(jnp.dot(normed2, w_g, preferred_element_type=jnp.float32), 'wd', wd_count)
        up_sum = token_sum(jnp.dot(normed2, w_u, preferred_element_type=jnp.float32), 'wd', wd_count)
        inner_rows = (jax.nn.gelu(gate_sum + bias_g.astype(jnp.float32), approximate=True) * (up_sum + bias_u.astype(jnp.float32))).astype(jnp.bfloat16)
        inner = lax.all_gather(inner_rows, 'wd', axis=0, tiled=True)
        down_sum = token_sum(jnp.dot(inner, w_d, preferred_element_type=jnp.float32), 'ch', ch_count)
        out_rows = (resid + down_sum + bias_d.astype(jnp.float32)).astype(jnp.bfloat16)
        return lax.all_gather(out_rows, 'ch', axis=0, tiled=True)

    return jax.shard_map(local_layer, mesh=mesh, in_specs=specs, out_specs=row_spec, check_vma=False)
```

profile of v0, /device:TPU:97, one launch (start us, length us, event | category | flops | bytes accessed | tf_op | source)
XLA Modules:
  0.0 2104.1 jit_solution(67861091182781582)
XLA Ops:
  9.9 24.0 %psum.14 = f32[4096,1]{0,1:T(1,128)S(1)} all-reduce(f32[4096,1]{0,1:T(1,128)S(1)} %bitcast.56), channel_id=1, replica_groups=mesh['dp'=1,'ch'=4,'wd'=8] {'wd'}, use_global_device_ids=true, to_apply=%region_1.0 | all-reduce | flops 4096 | bytes 32768 | tf_op jit(solution)/shard_map/psum | solution.py:62
  52.5 93.6 %all-to-all-done = bf16[8,512,1024]{2,1,0:T(8,128)(2,1)} async-done(((bf16[8,512,1024]{2,1,0:T(8,128)(2,1)}), bf16[8,512,1024]{2,1,0:T(8,128)(2,1)}, u32[]{:S(2)}, u32[]{:S(2)}) %all-to-all-start) | async-done | bytes 8388640 | tf_op jit(solution)/shard_map/all_to_all | solution.py:16
  168.4 121.7 %all-to-all-done.1 = bf16[8,512,1024]{2,1,0:T(8,128)(2,1)} async-done(((bf16[8,512,1024]{2,1,0:T(8,128)(2,1)}), bf16[8,512,1024]{2,1,0:T(8,128)(2,1)}, u32[]{:S(2)}, u32[]{:S(2)}) %all-to-all-start.1) | async-done | bytes 8388640 | tf_op jit(solution)/shard_map/all_to_all | solution.py:16
  320.2 11.3 slice.399
  331.5 24.6 %add_convert_fusion = bf16[4096,1024]{1,0:T(8,128)(2,1)} fusion(f32[4093,1024]{1,0:T(8,128)} %slice.403, f32[4094,1024]{1,0:T(8,128)} %slice.401, f32[4095,1024]{1,0:T(8,128)} %slice.399, f32[1024]{0:T(1024)S(1)} %bitcast.64, f32[1024]{0:T(1024)S(1)} %bitcast.63, f32[1024]{0:T(1024)S(1)} %bitcast.62, f32[1024]{0:T(1024)S(1)} %bitcast.61, ...), kind=kLoop, calls=%fused_computation.9 | loop fusion | flops 54525952 | bytes 67117056 | tf_op jit(solution)/shard_map/convert_element_type | solution.py:27
  356.1 11.7 copy.30
  367.8 11.5 fusion.50
  379.4 17.5 copy.37
  396.9 14.2 exponential_select_fusion
  411.1 36.7 %slice.308 = f32[1,2047,1024]{2,1,0:T(8,128)} slice(f32[1,4096,1024]{2,1,0:T(8,128)} %exponential_select_fusion), slice={[0:1:1], [2:4096:2], [0:1024:1]} | slice | bytes 16769024 | tf_op jit(solution)/shard_map/slice | solution.py:46
  447.7 36.0 %slice.313 = f32[1,2048,1024]{2,1,0:T(8,128)} slice(f32[1,4096,1024]{2,1,0:T(8,128)} %exponential_select_fusion), slice={[0:1:1], [0:4095:2], [0:1024:1]} | slice | bytes 16777216 | tf_op jit(solution)/shard_map/slice | solution.py:46
  483.8 36.1 %slice.309 = f32[1,2048,1024]{2,1,0:T(8,128)} slice(f32[1,4096,1024]{2,1,0:T(8,128)} %exponential_select_fusion), slice={[0:1:1], [1:4096:2], [0:1024:1]} | slice | bytes 16777216 | tf_op jit(solution)/shard_map/slice | solution.py:46
  519.8 11.5 fusion.51
  531.3 17.5 copy.36
  548.8 17.5 copy.33
  566.3 25.8 %multiply_bitcast_fusion = f32[1,4096,1024]{2,1,0:T(8,128)} fusion(bf16[4096,1024]{1,0:T(8,128)(2,1)} %add_convert_fusion, f32[4096,1024]{1,0:T(8,128)} %copy.36, f32[4096,1024]{1,0:T(8,128)} %copy.33, f32[1024]{0:T(1024)S(1)} %convert_element_type.126, f32[1024]{0:T(1024)S(1)} %fusion.35, f32[1024]{0:T(1024)S(1)} %convert_element_type.125, ...), kind=kLoop, calls=%fused_computation.8 | loop fusion | flops 62914560 | bytes 58736640 | tf_op jit(solution)/shard_map/reshape | solution.py:46
  592.1 36.6 %slice.397 = f32[1,2047,1024]{2,1,0:T(8,128)} slice(f32[1,4096,1024]{2,1,0:T(8,128)} %multiply_bitcast_fusion), slice={[0:1:1], [2:4096:2], [0:1024:1]} | slice | bytes 16769024 | tf_op jit(solution)/shard_map/slice | solution.py:46
  628.7 36.0 %slice.311 = f32[1,2048,1024]{2,1,0:T(8,128)} slice(f32[1,4096,1024]{2,1,0:T(8,128)} %multiply_bitcast_fusion), slice={[0:1:1], [1:4096:2], [0:1024:1]} | slice | bytes 16777216 | tf_op jit(solution)/shard_map/slice | solution.py:46
  664.7 36.0 %slice.310 = f32[1,2048,1024]{2,1,0:T(8,128)} slice(f32[1,4096,1024]{2,1,0:T(8,128)} %multiply_bitcast_fusion), slice={[0:1:1], [0:4095:2], [0:1024:1]} | slice | bytes 16777216 | tf_op jit(solution)/shard_map/slice | solution.py:46
  700.8 18.7 fusion.37
  719.5 18.5 slice.319
  738.0 18.5 slice.315
  756.5 18.5 slice.317
  775.0 18.5 slice.316
  793.5 12.2 fusion.38
  982.4 18.8 slice.395
  1001.3 19.0 slice.314
  1064.5 16.5 pad.106
  1081.0 16.7 pad.107
  1104.6 32.5 %pad.109 = f32[1,2048,1024]{2,1,0:T(8,128)} pad(f32[1,1024,1024]{2,1,0:T(8,128)} %add.370, f32[]{:T(128)} %constant.21.clone.1), padding=0_0_0x1_0_1x0_0_0 | pad | bytes 12582916 | tf_op jit(solution)/shard_map/pad | solution.py:46
  1147.4 32.4 %pad.108 = f32[1,2048,1024]{2,1,0:T(8,128)} pad(f32[1,1024,1024]{2,1,0:T(8,128)} %pad_maximum_fusion.1, f32[]{:T(128)} %constant.21.clone.1), padding=0_0_0x0_1_1x0_0_0 | pad | bytes 12582916 | tf_op jit(solution)/shard_map/pad | solution.py:46
  1179.8 12.0 add.372
  1191.8 12.7 fusion.3
  1208.8 64.2 %pad.110 = f32[1,4096,1024]{2,1,0:T(8,128)} pad(f32[1,2048,1024]{2,1,0:T(8,128)} %pad_maximum_fusion, f32[]{:T(128)} %constant.21.clone.1), padding=0_0_0x0_1_1x0_0_0 | pad | bytes 25165828 | tf_op jit(solution)/shard_map/pad | solution.py:46
  1273.0 64.1 %pad.111 = f32[1,4096,1024]{2,1,0:T(8,128)} pad(f32[1,2048,1024]{2,1,0:T(8,128)} %add.372, f32[]{:T(128)} %constant.21.clone.1), padding=0_0_0x1_0_1x0_0_0 | pad | bytes 25165828 | tf_op jit(solution)/shard_map/pad | solution.py:46
  1337.1 19.2 fusion.4
  1366.1 31.7 %all-to-all-done.2 = bf16[4,1024,384]{2,1,0:T(8,128)(2,1)} async-done(((bf16[4,1024,384]{2,1,0:T(8,128)(2,1)}), bf16[4,1024,384]{2,1,0:T(8,128)(2,1)}, u32[]{:S(2)}, u32[]{:S(2)}) %all-to-all-start.2) | async-done | bytes 3145760 | tf_op jit(solution)/shard_map/all_to_all | solution.py:16
  1402.2 13.5 psum.15
  1416.8 33.9 %all-gather.10.cloned.1.call-done = bf16[4096,384]{1,0:T(8,128)(2,1)} async-done(((bf16[1024,384]{1,0:T(8,128)(2,1)}), bf16[4096,384]{1,0:T(8,128)(2,1)}) %all-gather.10.cloned.1.call-update) | async-done | bytes 3145744 | tf_op jit(solution)/shard_map/all_gather | solution.py:77
  1450.7 15.2 convolution_convert_fusion
  1472.6 15.7 convolution_convert_fusion.1
  1488.4 190.2 %all-to-all-done.4 = bf16[8,512,2304]{2,1,0:T(8,128)(2,1)} async-done(((bf16[8,512,2304]{2,1,0:T(8,128)(2,1)}), bf16[8,512,2304]{2,1,0:T(8,128)(2,1)}, u32[]{:S(2)}, u32[]{:S(2)}) %all-to-all-start.4) | async-done | bytes 18874400 | tf_op jit(solution)/shard_map/all_to_all | solution.py:16
  1685.6 12.6 convert_reduce_fusion
  1698.2 193.3 %all-to-all-done.3 = bf16[8,512,2304]{2,1,0:T(8,128)(2,1)} async-done(((bf16[8,512,2304]{2,1,0:T(8,128)(2,1)}), bf16[8,512,2304]{2,1,0:T(8,128)(2,1)}, u32[]{:S(2)}, u32[]{:S(2)}) %all-to-all-start.3) | async-done | bytes 18874400 | tf_op jit(solution)/shard_map/all_to_all | solution.py:16
  1905.3 90.8 %all-gather.12.cloned.1.call-done = bf16[4096,2304]{1,0:T(8,128)(2,1)} async-done(((bf16[512,2304]{1,0:T(8,128)(2,1)}), bf16[4096,2304]{1,0:T(8,128)(2,1)}) %all-gather.12.cloned.1.call-update) | async-done | bytes 18874384 | tf_op jit(solution)/shard_map/all_gather | solution.py:81
  1996.1 15.5 convolution_convert_fusion.4
  2016.5 37.1 %all-to-all-done.5 = bf16[4,1024,384]{2,1,0:T(8,128)(2,1)} async-done(((bf16[4,1024,384]{2,1,0:T(8,128)(2,1)}), bf16[4,1024,384]{2,1,0:T(8,128)(2,1)}, u32[]{:S(2)}, u32[]{:S(2)}) %all-to-all-start.5) | async-done | bytes 3145760 | tf_op jit(solution)/shard_map/all_to_all | solution.py:16
  2057.3 36.0 %all-gather.14.cloned.1.call-done = bf16[4096,384]{1,0:T(8,128)(2,1)} async-done(((bf16[1024,384]{1,0:T(8,128)(2,1)}), bf16[4096,384]{1,0:T(8,128)(2,1)}) %all-gather.14.cloned.1.call-update) | async-done | bytes 3145744 | tf_op jit(solution)/shard_map/all_gather | solution.py:84
  (255 shorter events, 371.4 us)
Async XLA Ops:
  6.5 1444.1 %copy-start = (bf16[384,2304]{1,0:T(8,128)(2,1)S(1)}, bf16[384,2304]{1,0:T(8,128)(2,1)}, u32[]{:S(2)}) copy-start(bf16[384,2304]{1,0:T(8,128)(2,1)} %param.42) | copy-start | bytes 5308420
  43.9 8.5 copy-start.33
  43.9 102.1 %all-to-all-start = ((bf16[8,512,1024]{2,1,0:T(8,128)(2,1)}), bf16[8,512,1024]{2,1,0:T(8,128)(2,1)}, u32[]{:S(2)}, u32[]{:S(2)}) async-start(bf16[8,512,1024]{2,1,0:T(8,128)(2,1)} %bitcast.54), calls=%async_computation | async-start | bytes 16777216 | tf_op jit(solution)/shard_map/all_to_all | solution.py:16
  52.5 245.2 %all-gather.6.cloned.1.call-start = ((), (), s32[]{:S(2)}) async-start(), calls=%async_computation.6 | async-start | bytes 9437184 | tf_op jit(solution)/shard_map/all_gather | solution.py:69
  52.5 100.6 %copy-start.41 = (bf16[384,1024]{1,0:T(8,128)(2,1)S(1)}, bf16[384,1024]{1,0:T(8,128)(2,1)}, u32[]{:S(2)}) copy-start(bf16[384,1024]{1,0:T(8,128)(2,1)} %param.28) | copy-start | bytes 2359300
  161.8 6.3 copy-start.34
  161.8 6.3 copy-start.35
  161.8 6.4 copy-start.36
  161.8 6.4 copy-start.37
  161.8 6.4 copy-start.29
  161.8 6.6 copy-start.32
  161.8 6.6 copy-start.17
  161.8 128.3 %all-to-all-start.1 = ((bf16[8,512,1024]{2,1,0:T(8,128)(2,1)}), bf16[8,512,1024]{2,1,0:T(8,128)(2,1)}, u32[]{:S(2)}, u32[]{:S(2)}) async-start(bf16[8,512,1024]{2,1,0:T(8,128)(2,1)} %bitcast.53), calls=%async_computation.1 | async-start | bytes 16777216 | tf_op jit(solution)/shard_map/all_to_all | solution.py:16
  167.9 1169.2 %all-gather.8.cloned.1.call-start = ((), (), s32[]{:S(2)}) async-start(), calls=%async_computation.7 | async-start | bytes 9437184 | tf_op jit(solution)/shard_map/all_gather | solution.py:66
  356.1 11.7 copy-start.6
  483.8 36.1 %copy-start.7 = (bf16[4,256,256]{2,1,0:T(8,128)(2,1)S(1)}, bf16[4,256,256]{2,1,0:T(8,128)(2,1)}, u32[]{:S(2)}) copy-start(bf16[4,256,256]{2,1,0:T(8,128)(2,1)} %param.35) | copy-start | bytes 1572868
  1001.2 21.9 %copy-start.16 = (f32[1,2,1024]{2,1,0:T(2,128)S(1)}, f32[1,2,1024]{2,1,0:T(2,128)}, u32[]{:S(2)}) copy-start(f32[1,2,1024]{2,1,0:T(2,128)} %slice.369) | copy-start | bytes 24580
  1001.2 21.9 %copy-start.18 = (f32[1,2,1024]{2,1,0:T(2,128)S(1)}, f32[1,2,1024]{2,1,0:T(2,128)}, u32[]{:S(2)}) copy-start(f32[1,2,1024]{2,1,0:T(2,128)} %slice.371) | copy-start | bytes 24580
  1001.2 21.9 %copy-start.19 = (f32[1,2,1024]{2,1,0:T(2,128)S(1)}, f32[1,2,1024]{2,1,0:T(2,128)}, u32[]{:S(2)}) copy-start(f32[1,2,1024]{2,1,0:T(2,128)} %slice.370) | copy-start | bytes 24580
  1001.2 21.9 %copy-start.20 = (f32[1,2,1024]{2,1,0:T(2,128)S(1)}, f32[1,2,1024]{2,1,0:T(2,128)}, u32[]{:S(2)}) copy-start(f32[1,2,1024]{2,1,0:T(2,128)} %slice.373) | copy-start | bytes 24580
  1001.2 22.8 %copy-start.14 = (f32[1,3,1024]{2,1,0:T(4,128)S(1)}, f32[1,3,1024]{2,1,0:T(4,128)}, u32[]{:S(2)}) copy-start(f32[1,3,1024]{2,1,0:T(4,128)} %slice.379) | copy-start | bytes 36868
  1001.2 22.8 %copy-start.15 = (f32[1,3,1024]{2,1,0:T(4,128)S(1)}, f32[1,3,1024]{2,1,0:T(4,128)}, u32[]{:S(2)}) copy-start(f32[1,3,1024]{2,1,0:T(4,128)} %slice.362) | copy-start | bytes 36868
  1001.2 22.8 %copy-start.28 = (f32[1,1,1024]{2,1,0:T(1,128)S(1)}, f32[1,1,1024]{2,1,0:T(1,128)}, u32[]{:S(2)}) copy-start(f32[1,1,1024]{2,1,0:T(1,128)} %slice.414) | copy-start | bytes 12292
  1001.3 22.9 %copy-start.12 = (f32[1,7,1024]{2,1,0:T(8,128)S(1)}, f32[1,7,1024]{2,1,0:T(8,128)}, u32[]{:S(2)}) copy-start(f32[1,7,1024]{2,1,0:T(8,128)} %slice.356) | copy-start | bytes 86020
  1001.3 22.9 %copy-start.13 = (f32[1,7,1024]{2,1,0:T(8,128)S(1)}, f32[1,7,1024]{2,1,0:T(8,128)}, u32[]{:S(2)}) copy-start(f32[1,7,1024]{2,1,0:T(8,128)} %slice.381) | copy-start | bytes 86020
  1001.3 22.9 %copy-start.27 = (f32[1,1,1024]{2,1,0:T(1,128)S(1)}, f32[1,1,1024]{2,1,0:T(1,128)}, u32[]{:S(2)}) copy-start(f32[1,1,1024]{2,1,0:T(1,128)} %slice.413) | copy-start | bytes 12292
  1001.3 23.0 %copy-start.11 = (f32[1,15,1024]{2,1,0:T(8,128)S(1)}, f32[1,15,1024]{2,1,0:T(8,128)}, u32[]{:S(2)}) copy-start(f32[1,15,1024]{2,1,0:T(8,128)} %slice.350) | copy-start | bytes 184324
  1001.3 23.0 %copy-start.26 = (f32[1,1,1024]{2,1,0:T(1,128)S(1)}, f32[1,1,1024]{2,1,0:T(1,128)}, u32[]{:S(2)}) copy-start(f32[1,1,1024]{2,1,0:T(1,128)} %slice.412) | copy-start | bytes 12292
  1001.3 23.1 %copy-start.9 = (f32[1,31,1024]{2,1,0:T(8,128)S(1)}, f32[1,31,1024]{2,1,0:T(8,128)}, u32[]{:S(2)}) copy-start(f32[1,31,1024]{2,1,0:T(8,128)} %slice.344) | copy-start | bytes 380932
  1001.3 23.1 %copy-start.10 = (f32[1,31,1024]{2,1,0:T(8,128)S(1)}, f32[1,31,1024]{2,1,0:T(8,128)}, u32[]{:S(2)}) copy-start(f32[1,31,1024]{2,1,0:T(8,128)} %slice.385) | copy-start | bytes 380932
  1001.3 23.1 %copy-start.25 = (f32[1,1,1024]{2,1,0:T(1,128)S(1)}, f32[1,1,1024]{2,1,0:T(1,128)}, u32[]{:S(2)}) copy-start(f32[1,1,1024]{2,1,0:T(1,128)} %slice.411) | copy-start | bytes 12292
  1020.3 10.5 copy-start.5
  1032.9 17.9 copy-start.24
  1137.0 7.9 copy-start.22
  1191.8 12.7 copy-start.21
  1273.0 64.1 %copy-start.8 = (bf16[1024,384]{1,0:T(8,128)(2,1)S(1)}, bf16[1024,384]{1,0:T(8,128)(2,1)}, u32[]{:S(2)}) copy-start(bf16[1024,384]{1,0:T(8,128)(2,1)} %param.37) | copy-start | bytes 2359300
  1356.3 41.5 %all-to-all-start.2 = ((bf16[4,1024,384]{2,1,0:T(8,128)(2,1)}), bf16[4,1024,384]{2,1,0:T(8,128)(2,1)}, u32[]{:S(2)}, u32[]{:S(2)}) async-start(bf16[4,1024,384]{2,1,0:T(8,128)(2,1)} %bitcast.52), calls=%async_computation.2 | async-start | bytes 6291456 | tf_op jit(solution)/shard_map/all_to_all | solution.py:16
  1361.1 5.0 copy-start.38
  1361.1 5.0 copy-start.39
  1361.1 89.6 %all-gather.10.cloned.1.call-start = ((), (), s32[]{:S(2)}) async-start(), calls=%async_computation.8 | async-start | bytes 3932160 | tf_op jit(solution)/shard_map/all_gather | solution.py:77
  1465.9 212.7 %all-to-all-start.4 = ((bf16[8,512,2304]{2,1,0:T(8,128)(2,1)}), bf16[8,512,2304]{2,1,0:T(8,128)(2,1)}, u32[]{:S(2)}, u32[]{:S(2)}) async-start(bf16[8,512,2304]{2,1,0:T(8,128)(2,1)} %bitcast.51), calls=%async_computation.4 | async-start | bytes 37748736 | tf_op jit(solution)/shard_map/all_to_all | solution.py:16
  1678.6 7.0 copy-start.30
  1678.6 7.0 copy-start.31
  1678.6 213.0 %all-to-all-start.3 = ((bf16[8,512,2304]{2,1,0:T(8,128)(2,1)}), bf16[8,512,2304]{2,1,0:T(8,128)(2,1)}, u32[]{:S(2)}, u32[]{:S(2)}) async-start(bf16[8,512,2304]{2,1,0:T(8,128)(2,1)} %bitcast.50), calls=%async_computation.3 | async-start | bytes 37748736 | tf_op jit(solution)/shard_map/all_to_all | solution.py:16
  1685.6 310.5 %all-gather.12.cloned.1.call-start = ((), (), s32[]{:S(2)}) async-start(), calls=%async_computation.9 | async-start | bytes 21233664 | tf_op jit(solution)/shard_map/all_gather | solution.py:81
  1891.6 10.6 copy-start.3
  2011.5 42.1 %all-to-all-start.5 = ((bf16[4,1024,384]{2,1,0:T(8,128)(2,1)}), bf16[4,1024,384]{2,1,0:T(8,128)(2,1)}, u32[]{:S(2)}, u32[]{:S(2)}) async-start(bf16[4,1024,384]{2,1,0:T(8,128)(2,1)} %bitcast.55), calls=%async_computation.5 | async-start | bytes 6291456 | tf_op jit(solution)/shard_map/all_to_all | solution.py:16
  2016.4 76.8 %all-gather.14.cloned.1.call-start = ((), (), s32[]{:S(2)}) async-start(), calls=%async_computation.10 | async-start | bytes 3932160 | tf_op jit(solution)/shard_map/all_gather | solution.py:84
  (5 other events, 20.7 us)
Sparse Core Ops, SparseCore 0:
  153.2 88.5 all-gather.5
  297.7 47.4 all-gather.7
  1416.9 33.7 all-gather.9
  1905.4 90.6 all-gather.11
  2057.4 35.8 all-gather.13
where the time goes:
time: 2130 us; the launch traced here: 2100 us
  local copies, waits for them, and re-layouts  837 us (39%)
  waiting for transfers between devices  829 us (39%)
  other arithmetic  241 us (11%)
  matrix products  107 us (5%)
  starting transfers between devices  38.3 us (2%)
  blocking collectives  37.5 us (2%)
    all_to_all x6, waiting for transfers between devices, token_sum(): received = lax.all_to_all(pieces, axis_name, 0, 0)  668 us
    slice x74, local copies, waits for them, and re-layouts, rg_lru(): lax.associative_scan(combine, (decay.reshape(seqs, steps, width), drive.r...  487 us
    pad x22, local copies, waits for them, and re-layouts, rg_lru(): lax.associative_scan(combine, (decay.reshape(seqs, steps, width), drive.r...  247 us
    all_gather x1, waiting for transfers between devices, local_layer(): inner = lax.all_gather(inner_rows, 'wd', axis=0, tiled=True)  90.8 us
    mul x10, other arithmetic, combine(): return (left[0] * right[0], right[0] * left[1] + right[1])  52.1 us
  transfers between devices with their start and end apart: 11, of which 9 were waited for; matrix products, arithmetic and copies ran while one was open for 52% of the time, Pallas kernels for 0%

commit v1 on v0

v1 whole, which is shorter than its diff:
```python
import functools

import jax
import jax.numpy as jnp
from jax import lax
from jax.experimental import pallas as pl
from jax.experimental.pallas import tpu as pltpu
from jax.sharding import PartitionSpec as P

EPS = 1e-6
F32 = jnp.float32
BF16 = jnp.bfloat16
MESH = pl.DeviceIdType.MESH
VMEM = pltpu.VMEM
ANY = pl.ANY
HALO = 16
TILE = 8
VMEM_LIMIT = 62 * 1024 * 1024
HOPS = ((0, 0), (0, 1), (-1, 0), (1, 0), (-1, 1), (1, 1), (2, 0), (2, 1))


def remote(src, dst, send, recv, **to):
    return pltpu.make_async_remote_copy(src_ref=src, dst_ref=dst, send_sem=send, recv_sem=recv, device_id=to, device_id_type=MESH)


def shifted(index, by, count):
    return lax.rem(index + (by % count), count)


def rms(vals, sum_sq, width, gain):
    return (vals * lax.rsqrt(sum_sq / width + EPS) * (1.0 + gain)).astype(BF16)


def aligned(start, size):
    return pl.ds(pl.multiple_of(start, size), size)


def ring_gather(buf, c, nc, rows, send, recv):
    right, left = shifted(c, 1, nc), shifted(c, -1, nc)
    half = rows // 2

    def make(block, part, to, k):
        piece = buf.at[aligned(block * rows + part * half, half)]
        return remote(piece, piece, send.at[k], recv.at[k], ch=to)

    own = [make(c, 0, right, 0), make(c, 1, left, 1), make(c, 1, right, 2), make(c, 0, left, 3)]
    relay = [make(left, 0, right, 4), make(right, 1, left, 5)]

    def begin():
        for copy in own:
            copy.start()

    def middle():
        for copy, onward in zip(own[:2], relay):
            copy.wait_recv()
            onward.start()

    def end():
        for copy in own[2:] + relay:
            copy.wait_recv()
        for copy in own + relay:
            copy.wait_send()

    return begin, middle, end


def ring_sums(c, nc, rows, pbuf, sbuf, far_r, far_l, near_r, near_l, send, recv):
    right, left = shifted(c, 1, nc), shifted(c, -1, nc)
    opposite = shifted(c, 2, nc)
    half = rows // 2

    def at(block, part=None):
        if part is None:
            return aligned(block * rows, rows)
        return aligned(block * rows + part * half, half)

    def far(k):
        return (remote(sbuf.at[k, at(opposite, 0)], far_r.at[k], send.at[0, k], recv.at[0, k], ch=right),
                remote(sbuf.at[k, at(opposite, 1)], far_l.at[k], send.at[1, k], recv.at[1, k], ch=left))

    def near(k):
        return (remote(sbuf.at[k, at(right)], near_r.at[k], send.at[2, k], recv.at[2, k], ch=right),
                remote(sbuf.at[k, at(left)], near_l.at[k], send.at[3, k], recv.at[3, k], ch=left))

    def first(k, partial):
        pbuf[k] = partial
        sbuf[k] = partial.astype(BF16)
        for copy in far(k):
            copy.start()

    def second(k):
        to_right, to_left = far(k)
        onward = near(k)
        to_right.wait_recv()
        sbuf[k, at(right, 0)] = (pbuf[k, at(right, 0)] + far_r[k].astype(F32)).astype(BF16)
        onward[0].start()
        to_left.wait_recv()
        sbuf[k, at(left, 1)] = (pbuf[k, at(left, 1)] + far_l[k].astype(F32)).astype(BF16)
        onward[1].start()

    def third(k):
        for copy in near(k):
            copy.wait_recv()
        return pbuf[k, at(c)] + near_r[k].astype(F32) + near_l[k].astype(F32)

    def drain(k):
        for copy in far(k) + near(k):
            copy.wait_send()

    return first, second, third, drain


def layer_kernel(nw, nc, x_ref, seg_ref, wx, wy, wo, wg, wu, wd, gt_ref, bo_ref, gm_ref, bd_ref, bx_ref, by_ref, cb_ref, rb_ref, ib_ref, lam_ref, cw_ref, rg_ref, ig_ref, bg_ref, bu_ref,
                 out_ref, wx_all, wy_all, wo_all, wg_all, wu_all, wd_all,
                 xbuf, pbufs, pv_ref, pos_ref, wide_ref, xown, pars, nall, mall, wtile, ctile, stage_r, stage_c, ubuf, hsend, hrecv, ybuf, abuf, bbuf, tot, mixed, gbuf, inner, res,
                 pbuf, sbuf, far_r, far_l, near_r, near_l, osend, fin,
                 lsem, tsem, csem, outsem, xs, xr, ps, pr, ns, nr, hs, hr, ts, tr, as_, ar, ms, mr, ds, dr, os_, or_, fs, fr, ss, rs):
    w, c = lax.axis_index('wd'), lax.axis_index('ch')
    nx = nw // 2
    chip, core = w // 2, w % 2
    rows, part = xown.shape[0], xbuf.shape[2]
    tokens, chans = ybuf.shape
    width = part * nw

    def member(step, other):
        return shifted(chip, step, nx) * 2 + (core + other) % 2

    right_w, left_w, far_w, mate = member(1, 0), member(-1, 0), member(2, 0), member(0, 1)

    barrier = pltpu.get_barrier_semaphore()
    for d in range(1, nw):
        pl.semaphore_signal(barrier, inc=1, device_id={'wd': shifted(w, d, nw)}, device_id_type=MESH)
    for d in (1, -1):
        pl.semaphore_signal(barrier, inc=1, device_id={'ch': shifted(c, d, nc)}, device_id_type=MESH)
    pl.semaphore_wait(barrier, nw + 1)

    weights = ((wx, wx_all), (wy, wy_all), (wo, wo_all), (wg, wg_all), (wu, wu_all), (wd, wd_all))

    def stream(i):
        src, dst = weights[i]
        depth = src.shape[0]
        half = depth // 2

        def piece(block, k):
            return dst.at[aligned(block * depth + k * half, half)]

        low, high = src.at[pl.ds(0, half)], src.at[pl.ds(half, half)]
        mine = dst.at[aligned(w * depth, depth)]
        first_sends = ((low, piece(w, 0), right_w), (high, piece(w, 1), left_w), (high, piece(w, 1), right_w), (low, piece(w, 0), left_w), (src, mine, mate))
        relays = ((left_w, 0, right_w), (right_w, 1, left_w), (left_w, 0, mate), (right_w, 1, mate), (left_w, 1, mate), (right_w, 0, mate), (far_w, 0, mate), (far_w, 1, mate))

        def copy(k):
            if k < len(first_sends):
                source, target, to = first_sends[k]
            else:
                block, p, to = relays[k - len(first_sends)]
                source = target = piece(block, p)
            return remote(source, target, ss.at[i, k], rs.at[i, k], wd=to)

        if depth == part:
            stage = stage_r.at[:, pl.ds(0, src.shape[1])]
        else:
            stage = stage_c.at[pl.ds(0, depth)]

        def load():
            return pltpu.make_async_copy(src, stage, lsem.at[0])

        def keep():
            return pltpu.make_async_copy(stage, mine, lsem.at[1])

        return copy, load, keep

    def send_own(i):
        copy, load, keep = stream(i)
        for k in range(5):
            copy(k).start()
        load().start()
        load().wait()
        keep().start()

    def send_on(i):
        copy, load, keep = stream(i)
        keep().wait()
        copy(0).wait_recv()
        copy(5).start()
        copy(7).start()
        copy(1).wait_recv()
        copy(6).start()
        copy(8).start()

    def send_on_and_next(i):
        send_on(i)
        send_own(i + 1)

    def ready(i):
        copy = stream(i)[0]
        for k, onward in ((2, 9), (3, 10), (5, 11), (6, 12)):
            copy(k).wait_recv()
            copy(onward).start()
        for k in (4, 7, 8, 9, 10, 11, 12):
            copy(k).wait_recv()

    def column_tiles(src, body):
        size = wtile.shape[2]
        count = src.shape[1] // size

        def load(j, slot):
            return pltpu.make_async_copy(src.at[:, aligned(j * size, size)], wtile.at[slot], tsem.at[slot])

        load(0, 0).start()

        def step(j, carry):
            slot = lax.rem(j, 2)

            @pl.when(j + 1 < count)
            def _():
                load(j + 1, 1 - slot).start()

            load(j, slot).wait()
            body(aligned(j * size, size), wtile[slot])
            return carry

        lax.fori_loop(0, count, step, 0)

    def rows_of(t):
        return x_ref.at[aligned((t * nc + c) * rows, rows)]

    def wide_row(ref):
        return ref[...].astype(F32)[None, :]

    for k, ref in enumerate((gt_ref, bo_ref, gm_ref, bd_ref)):
        pbufs[w, k:k + 1, :] = wide_row(ref)
    pbufs[w, 4:, :] = jnp.zeros((4, part), F32)
    own = pltpu.make_async_copy(rows_of(w), xbuf.at[w], lsem.at[2])
    own.start()
    copies = []
    for d in range(1, nw):
        t = shifted(w, d, nw)
        copies.append(remote(rows_of(t), xbuf.at[w], xs.at[d], xr.at[d], wd=t))
        copies.append(remote(pbufs.at[w], pbufs.at[w], ps.at[d], pr.at[d], wd=t))
    for copy in copies:
        copy.start()
    send_own(0)
    for k, ref in enumerate((bx_ref, by_ref, cb_ref, rb_ref, ib_ref)):
        pv_ref[k:k + 1, :] = wide_row(ref)
    lam = lam_ref[...][None, :]
    pv_ref[5:6, :] = -8.0 * (jnp.maximum(-lam, 0.0) + jnp.log1p(jnp.exp(-jnp.abs(lam))))
    pv_ref[6:10, :] = cw_ref[...].astype(F32)
    wide_ref[0:1, :] = wide_row(bg_ref)
    wide_ref[1:2, :] = wide_row(bu_ref)
    pos_row = seg_ref[0:1, aligned(w * tokens, tokens)].astype(F32)
    pos_cols = jnp.broadcast_to(pos_row, (128, tokens)).T.astype(jnp.int32)
    for k in range(pos_ref.shape[1] // 128):
        pos_ref[:, k * 128:(k + 1) * 128] = pos_cols
    own.wait()
    for copy in copies:
        copy.wait_recv()
    total = jnp.zeros((rows, 1), F32)
    for j in range(nw):
        vals = xbuf[j].astype(F32)
        total = total + jnp.sum(vals * vals, axis=1, keepdims=True)
    my_rows = aligned(c * rows, rows)
    for j in range(nw):
        cols = slice(j * part, (j + 1) * part)
        xown[:, cols] = xbuf[j]
        pars[:, cols] = pbufs[j]
        nall[my_rows, cols] = rms(xbuf[j].astype(F32), total, width, pbufs[j, 0:1])
    begin, middle, end = ring_gather(nall, c, nc, rows, ns, nr)
    begin()
    for copy in copies:
        copy.wait_send()
    send_on_and_next(0)
    middle()
    end()

    ready(0)

    def u_tile(cols, weight):
        u = jnp.dot(nall[...], weight, preferred_element_type=F32) + pv_ref[0:1, cols]
        ubuf[pl.ds(HALO, tokens), cols] = u.astype(BF16).astype(F32)

    column_tiles(wx_all, u_tile)
    hsend[...] = ubuf[pl.ds(tokens, HALO), :].astype(BF16)
    halo = remote(hsend, hrecv, hs.at[0], hr.at[0], wd=shifted(w, 1, nw))
    halo.start()
    send_on_and_next(1)
    ready(1)

    def y_tile(cols, weight):
        y = jnp.dot(nall[...], weight, preferred_element_type=F32) + pv_ref[1:2, cols]
        ybuf[:, cols] = jax.nn.gelu(y, approximate=True).astype(BF16)

    column_tiles(wy_all, y_tile)
    halo.wait()
    ubuf[pl.ds(0, HALO), :] = hrecv[...].astype(F32)
    blocks, bw = rg_ref.shape[0], rg_ref.shape[1]

    def gate_block(j, carry):
        cols = aligned(j * bw, bw)
        pos = pos_ref[...]
        conv = pv_ref[2:3, cols] + ubuf[pl.ds(HALO, tokens), cols] * pv_ref[6:7, cols]
        for k in range(1, 4):
            conv = conv + jnp.where(pos >= k, ubuf[pl.ds(HALO - k, tokens), cols], 0.0) * pv_ref[6 + k:7 + k, cols]
        conv = conv.astype(BF16)
        rate = jax.nn.sigmoid(jnp.dot(conv, rg_ref[j], preferred_element_type=F32) + pv_ref[3:4, cols])
        inflow = jax.nn.sigmoid(jnp.dot(conv, ig_ref[j], preferred_element_type=F32) + pv_ref[4:5, cols])
        log_a = rate * pv_ref[5:6, cols]
        a = jnp.exp(log_a)
        z = 2.0 * log_a
        series = 1.0 + z * (1.0 / 8.0)
        for k in range(7, 1, -1):
            series = 1.0 + z * series * (1.0 / k)
        gap = jnp.maximum(jnp.where(z > -0.5, -z * series, 1.0 - a * a), 0.0)
        root = jnp.where(gap > 0.0, gap * lax.rsqrt(jnp.where(gap > 0.0, gap, 1.0)), 0.0)
        reset = pos == 0
        abuf[:, cols] = jnp.where(reset, 0.0, a)
        bbuf[:, cols] = jnp.where(reset, 1.0, root) * inflow * conv.astype(F32)
        return carry

    lax.fori_loop(0, blocks, gate_block, 0)
    send_on(2)

    sub = lax.broadcasted_iota(jnp.int32, (TILE, chans), 0)

    def scan_tile(i, carry):
        a_in, h_in = carry
        at = aligned(i * TILE, TILE)
        a, b = abuf[at, :], bbuf[at, :]
        for d in (1, 2, 4):
            keep = sub >= d
            b = b + a * jnp.where(keep, pltpu.roll(b, d, 0), 0.0)
            a = a * jnp.where(keep, pltpu.roll(a, d, 0), 1.0)
        h = b + a * h_in
        a = a * a_in
        abuf[at, :] = a
        bbuf[at, :] = h
        return jnp.broadcast_to(a[TILE - 1:], a.shape), jnp.broadcast_to(h[TILE - 1:], h.shape)

    a_tot, h_tot = lax.fori_loop(0, tokens // TILE, scan_tile, (jnp.ones((TILE, chans), F32), jnp.zeros((TILE, chans), F32)))
    tot[w] = jnp.where(sub < TILE // 2, a_tot, h_tot)
    copies = []
    for d in range(1, nw):
        copies.append(remote(tot.at[w], tot.at[w], ts.at[d], tr.at[d], wd=shifted(w, d, nw)))
    for copy in copies:
        copy.start()
    send_own(3)
    for copy in copies:
        copy.wait_recv()
    h_in = jnp.zeros((1, chans), F32)
    for s in range(nw):
        h_in = jnp.where(s < w, tot[s, 0:1] * h_in + tot[s, TILE - 1:], h_in)
    for j in range(blocks):
        cols = slice(j * bw, (j + 1) * bw)
        hidden = bbuf[:, cols] + abuf[:, cols] * h_in[:, cols]
        mixed[:, cols] = (hidden * ybuf[:, cols].astype(F32)).astype(BF16)
    for copy in copies:
        copy.wait_send()

    ready(2)
    first, second, third, drain = ring_sums(c, nc, rows, pbuf, sbuf, far_r, far_l, near_r, near_l, as_, ar)

    def o_load(j, slot):
        return pltpu.make_async_copy(wo_all.at[aligned(j * chans, chans)], ctile.at[slot, pl.ds(0, chans)], csem.at[slot])

    o_load(0, 0).start()

    def o_step(k, carry):
        slot = lax.rem(k, 2)

        @pl.when(k + 1 < nw)
        def _():
            o_load(k + 1, 1 - slot).start()

        o_load(k, slot).wait()
        first(k, jnp.dot(mixed[...], ctile[slot, pl.ds(0, chans), :], preferred_element_type=F32))
        return carry

    def o_second(k, carry):
        second(k)
        return carry

    lax.fori_loop(0, nw, o_step, 0)
    lax.fori_loop(0, nw, o_second, 0)
    send_on_and_next(3)
    total = jnp.zeros((rows, 1), F32)
    for k in range(nw):
        cols = slice(k * part, (k + 1) * part)
        vals = xown[:, cols].astype(F32) + third(k) + pars[1:2, cols]
        res[:, cols] = vals
        total = total + jnp.sum(vals * vals, axis=1, keepdims=True)
    for k in range(nw):
        cols = slice(k * part, (k + 1) * part)
        mall[my_rows, cols] = rms(res[:, cols], total, width, pars[2:3, cols])
    begin, middle, end = ring_gather(mall, c, nc, rows, ms, mr)
    begin()

    def o_drain(k, carry):
        drain(k)
        return carry

    lax.fori_loop(0, nw, o_drain, 0)
    middle()
    end()

    ready(3)

    def g_tile(cols, weight):
        g = jnp.dot(mall[...], weight, preferred_element_type=F32) + wide_ref[0:1, cols]
        gbuf[:, cols] = jax.nn.gelu(g, approximate=True)

    column_tiles(wg_all, g_tile)
    send_on_and_next(4)
    ready(4)

    def i_tile(cols, weight):
        u = jnp.dot(mall[...], weight, preferred_element_type=F32) + wide_ref[1:2, cols]
        inner[:, cols] = (gbuf[:, cols] * u).astype(BF16)

    column_tiles(wu_all, i_tile)
    send_on(5)

    first, second, third, drain = ring_sums(c, nc, rows, pbuf, sbuf, far_r, far_l, near_r, near_l, ds, dr)
    right, left = shifted(c, 1, nc), shifted(c, -1, nc)
    half = rows // 2
    depth = wd.shape[0]

    def pick(d, options):
        value = options[0]
        for k in range(1, nw):
            value = jnp.where(d == k, options[k], value)
        return value

    targets = [member(step, other) for step, other in HOPS]
    sources = [member(-step, other) for step, other in HOPS]

    def block_of(d):
        return pick(d, targets)

    def source_of(d):
        return pick(d, sources)

    down = stream(5)[0]

    def arrived(d):
        needs = {1: ((4, None),), 2: ((2, 9), (3, 10)), 4: ((7, None), (9, None)), 5: ((8, None), (10, None)), 6: ((5, 11), (6, 12)), 7: ((11, None), (12, None))}
        for k, items in needs.items():
            @pl.when(d == k)
            def _():
                for index, onward in items:
                    down(index).wait_recv()
                    if onward is not None:
                        down(onward).start()

    def rows_at(owner, group, at=0, size=rows):
        return aligned((owner * nc + group) * rows + at, size)

    def hop(d):
        return remote(osend.at[d], fin.at[rows_at(w, c)], os_.at[d], or_.at[d], wd=block_of(d))

    def spread(d):
        piece = fin.at[rows_at(source_of(d), c)]
        return (remote(piece, piece, fs.at[0, d], fr.at[0, d], ch=right), remote(piece, piece, fs.at[1, d], fr.at[1, d], ch=left))

    def relay(d):
        from_left = fin.at[rows_at(source_of(d), left, 0, half)]
        from_right = fin.at[rows_at(source_of(d), right, half, half)]
        return (remote(from_left, from_left, fs.at[2, d], fr.at[2, d], ch=right), remote(from_right, from_right, fs.at[3, d], fr.at[3, d], ch=left))

    def finish(e):
        cols = aligned(block_of(e) * part, part)
        done = (res[:, cols] + third(e) + pars[3:4, cols]).astype(BF16)

        @pl.when(e == 0)
        def _():
            fin[rows_at(w, c), :] = done

        @pl.when(e > 0)
        def _():
            osend[e] = done
            hop(e).start()

    def share(e):
        @pl.when(e > 0)
        def _():
            hop(e).wait_recv()

        for copy in spread(e):
            copy.start()

    def pass_on(e):
        for copy, onward in zip(spread(e), relay(e)):
            copy.wait_recv()
            onward.start()

    def store(e):
        at = aligned(source_of(e) * tokens, tokens)
        return pltpu.make_async_copy(fin.at[at], out_ref.at[at], outsem.at[e])

    def complete(e):
        for copy in relay(e):
            copy.wait_recv()
        store(e).start()

    def d_step(d, carry):
        arrived(d)
        load = pltpu.make_async_copy(wd_all.at[aligned(block_of(d) * depth, depth)], ctile.at[0], csem.at[0])
        load.start()
        load.wait()
        first(d, jnp.dot(inner[...], ctile[0], preferred_element_type=F32))

        @pl.when(d >= 1)
        def _():
            second(d - 1)

        @pl.when(d >= 2)
        def _():
            finish(d - 2)

        for k in (0, 1):
            @pl.when(d == k + 4)
            def _():
                share(k)

            @pl.when(d == k + 6)
            def _():
                pass_on(k)

        return carry

    def each(first_one, last_one, body):
        def step(e, carry):
            body(e)
            return carry

        lax.fori_loop(first_one, last_one, step, 0)

    lax.fori_loop(0, nw, d_step, 0)
    second(nw - 1)
    finish(nw - 2)
    each(2, 4, share)
    finish(nw - 1)
    each(4, 6, share)
    each(2, 4, pass_on)
    share(6)
    each(4, 6, pass_on)
    share(7)
    each(6, 8, pass_on)
    each(0, nw, complete)

    def settle(d):
        for copy in spread(d) + relay(d):
            copy.wait_send()
        drain(d)

        @pl.when(d > 0)
        def _():
            hop(d).wait_send()

    each(0, nw, settle)
    for i in range(len(weights)):
        copy = stream(i)[0]
        for k in range(13):
            copy(k).wait_send()
    for k in range(nw):
        store(k).wait()


def dma(*shape):
    return pltpu.SemaphoreType.DMA(shape)


def solution(mesh):
    nw = mesh.shape['wd']
    nc = mesh.shape['ch']
    assert nc == 4 and nw == len(HOPS)
    row_spec = P('dp', 'wd')
    specs = (row_spec, P('dp', None), P('wd'), P('wd', 'ch'), P('ch'), P('wd', 'ch'), P('ch'), P(None, 'ch'), P('ch'), P('ch'), P('ch', None, None), P('ch'), P('ch', None, None), P('ch'), P('ch', 'wd'), P('wd'), P('wd'), P('wd', 'ch'), P('ch'), P('wd', 'ch'), P('ch'), P('ch', 'wd'), P('wd'))
    vm = pl.BlockSpec(memory_space=VMEM)
    anywhere = pl.BlockSpec(memory_space=ANY)

    def local_layer(resid_in, seg_pos, gain_temporal, w_x, bias_x, w_y, bias_y, conv_w, conv_bias, lam_param, rgate_w, rgate_b, igate_w, igate_b, w_o, bias_o, gain_mlp, w_g, bias_g, w_u, bias_u, w_d, bias_d):
        tokens, part = resid_in.shape
        width = part * nw
        span = tokens // nw
        rows = span // nc
        chans = w_x.shape[1]
        wide = w_g.shape[1]
        bw = rgate_w.shape[1]
        assert seg_pos.shape[0] == 1

        def landing(arr):
            return jax.ShapeDtypeStruct((arr.shape[0] * nw, arr.shape[1]), arr.dtype)

        stream = (w_x, w_y, w_o, w_g, w_u, w_d)
        scratch = [
            VMEM((nw, rows, part), BF16), VMEM((nw, 8, part), F32), VMEM((16, chans), F32), VMEM((span, bw), jnp.int32), VMEM((8, wide), F32), VMEM((rows, width), BF16), VMEM((8, width), F32),
            VMEM((span, width), BF16), VMEM((span, width), BF16), VMEM((2, width, bw), BF16), VMEM((2, wide, part), BF16),
            VMEM((part, wide), BF16), VMEM((wide, part), BF16),
            VMEM((span + HALO, chans), F32), VMEM((HALO, chans), BF16), VMEM((HALO, chans), BF16), VMEM((span, chans), BF16),
            VMEM((span, chans), F32), VMEM((span, chans), F32), VMEM((nw, TILE, chans), F32), VMEM((span, chans), BF16),
            VMEM((span, wide), F32), VMEM((span, wide), BF16), VMEM((rows, width), F32),
            VMEM((nw, span, part), F32), VMEM((nw, span, part), BF16), VMEM((nw, rows // 2, part), BF16), VMEM((nw, rows // 2, part), BF16),
            VMEM((nw, rows, part), BF16), VMEM((nw, rows, part), BF16), VMEM((nw, rows, part), BF16), VMEM((tokens, part), BF16),
            dma(4), dma(2), dma(2), dma(nw), dma(nw), dma(nw), dma(nw), dma(nw), dma(6), dma(6), dma(1), dma(1), dma(nw), dma(nw),
            dma(4, nw), dma(4, nw), dma(6), dma(6), dma(4, nw), dma(4, nw), dma(nw), dma(nw), dma(4, nw), dma(4, nw),
            dma(len(stream), 13), dma(len(stream), 13),
        ]
        return pl.pallas_call(
            functools.partial(layer_kernel, nw, nc), name='layer',
            out_shape=(jax.ShapeDtypeStruct((tokens, part), BF16),) + tuple(landing(arr) for arr in stream),
            in_specs=[anywhere] + [vm] + [anywhere] * 6 + [vm] * 15, out_specs=(anywhere,) * 7, scratch_shapes=scratch,
            compiler_params=pltpu.CompilerParams(vmem_limit_bytes=VMEM_LIMIT, collective_id=0, has_side_effects=True),
        )(resid_in, seg_pos, *stream, gain_temporal, bias_o, gain_mlp, bias_d, bias_x, bias_y, conv_bias, rgate_b, igate_b, lam_param, conv_w, rgate_w, igate_w, bias_g, bias_u)[0]

    return jax.shard_map(local_layer, mesh=mesh, in_specs=specs, out_specs=row_spec, check_vma=False)
```

time: 2130 us -> 314 us (0.15); the launches traced: 2100 us -> 313 us
  local copies, waits for them, and re-layouts: 837 us -> 3.87 us
  waiting for transfers between devices: 829 us -> 0 us
  Pallas kernels: 0 us -> 309 us
  other arithmetic: 241 us -> 0 us
  matrix products: 107 us -> 0 us
  starting transfers between devices: 38.3 us -> 0 us
  blocking collectives: 37.5 us -> 0 us
    all_to_all x6 -> x0, waiting for transfers between devices: 668 us -> none  [token_sum(): received = lax.all_to_all(pieces, axis_name, 0, 0)]
    slice x78 -> x0, local copies, waits for them, and re-layouts: 521 us -> none  [the longest x74 487 us: rg_lru(): lax.associative_scan(combine, (decay.reshape(seqs, steps, width), drive.r...]
    pallas_call x0 -> x1, Pallas kernels: none -> 309 us  [local_layer(): pl.pallas_call(functools.partial(layer_kernel, nw, nc), name='layer', out...]
    pad x22 -> x0, local copies, waits for them, and re-layouts: 247 us -> none  [rg_lru(): lax.associative_scan(combine, (decay.reshape(seqs, steps, width), drive.r...]
    all_gather x5 -> x0, waiting for transfers between devices: 161 us -> none  [the longest x1 90.8 us: local_layer(): inner = lax.all_gather(inner_rows, 'wd', axis=0, tiled=True)]
    dot_general x8 -> x0, matrix products: 107 us -> none  [the longest x1 19.2 us: local_layer(): jnp.dot(mixed, w_o, preferred_element_type=jnp.float32)]
    add x24 -> x0, other arithmetic: 55.8 us -> none  [the longest x11 27.7 us: combine(): return (left[0] * right[0], right[0] * left[1] + right[1])]
    reshape x3 -> x0, local copies, waits for them, and re-layouts: 52.4 us -> none  [the longest x2 35 us: rg_lru(): jnp.einsum('nbi,bij->nbj', grouped, rgate_w, preferred_element_type=jnp.f...]
  transfers between devices with their start and end apart: 11 -> 0, of which waited for: 9 -> 0; matrix products, arithmetic and copies ran while one was open for 52% -> 0% of each run, Pallas kernels for 0% -> 0%
where the time goes in v1:
time: 314 us; the launch traced here: 313 us
  Pallas kernels  309 us (98%)
  local copies, waits for them, and re-layouts  3.87 us (1%)
    pallas_call x1, Pallas kernels, local_layer(): pl.pallas_call(functools.partial(layer_kernel, nw, nc), name='layer', out...  309 us

profile of v1, /device:TPU:97, one launch (start us, length us, event | category | flops | bytes accessed | tf_op | source)
XLA Modules:
  0.0 312.6 jit_solution(1580252543521727265)
XLA Ops:
  0.0 308.7 %layer.1 = (bf16[4096,384]{1,0:T(8,128)(2,1)}, bf16[3072,1024]{1,0:T(8,128)(2,1)}, bf16[3072,1024]{1,0:T(8,128)(2,1)}, bf16[8192,384]{1,0:T(8,128)(2,1)}, bf16[3...) custom-call(bf16[4096,384]{1,0:T(8,128)(2,1)} %x_ref.1, s32[1,4096]{1,0:T(1,128)} %seg_ref.1, ...), custom_call_target="tpu_custom_call" | custom-call | tf_op jit(solution)/shard_map/layer/pallas_call | solution.py:608
  308.7 3.9 %copy.25 = bf16[4096,384]{1,0:T(8,128)(2,1)} copy(bf16[4096,384]{1,0:T(8,128)(2,1)} %get-tuple-element.6) | data formatting | bytes 6291456

commit v2 on v1

--- a/solution.py
+++ b/solution.py
@@ -8,6 +8,7 @@
 from jax.sharding import PartitionSpec as P
 
 EPS = 1e-6
+SLIM = 128
 F32 = jnp.float32
 BF16 = jnp.bfloat16
 MESH = pl.DeviceIdType.MESH
@@ -74,37 +75,42 @@
             return aligned(block * rows, rows)
         return aligned(block * rows + part * half, half)
 
-    def far(k):
-        return (remote(sbuf.at[k, at(opposite, 0)], far_r.at[k], send.at[0, k], recv.at[0, k], ch=right),
-                remote(sbuf.at[k, at(opposite, 1)], far_l.at[k], send.at[1, k], recv.at[1, k], ch=left))
-
-    def near(k):
-        return (remote(sbuf.at[k, at(right)], near_r.at[k], send.at[2, k], recv.at[2, k], ch=right),
-                remote(sbuf.at[k, at(left)], near_l.at[k], send.at[3, k], recv.at[3, k], ch=left))
-
-    def first(k, partial):
-        pbuf[k] = partial
-        sbuf[k] = partial.astype(BF16)
-        for copy in far(k):
+    def far(unit):
+        k, s, lanes = unit
+        return (remote(sbuf.at[k, at(opposite, 0), lanes], far_r.at[k, :, lanes], send.at[0, s], recv.at[0, s], ch=right),
+                remote(sbuf.at[k, at(opposite, 1), lanes], far_l.at[k, :, lanes], send.at[1, s], recv.at[1, s], ch=left))
+
+    def near(unit):
+        k, s, lanes = unit
+        return (remote(sbuf.at[k, at(right), lanes], near_r.at[k, :, lanes], send.at[2, s], recv.at[2, s], ch=right),
+                remote(sbuf.at[k, at(left), lanes], near_l.at[k, :, lanes], send.at[3, s], recv.at[3, s], ch=left))
+
+    def first(unit, partial):
+        k, s, lanes = unit
+        pbuf[k, :, lanes] = partial
+        sbuf[k, :, lanes] = partial.astype(BF16)
+        for copy in far(unit):
             copy.start()
 
-    def second(k):
-        to_right, to_left = far(k)
-        onward = near(k)
+    def second(unit):
+        k, s, lanes = unit
+        to_right, to_left = far(unit)
+        onward = near(unit)
         to_right.wait_recv()
-        sbuf[k, at(right, 0)] = (pbuf[k, at(right, 0)] + far_r[k].astype(F32)).astype(BF16)
+        sbuf[k, at(right, 0), lanes] = (pbuf[k, at(right, 0), lanes] + far_r[k, :, lanes].astype(F32)).astype(BF16)
         onward[0].start()
         to_left.wait_recv()
-        sbuf[k, at(left, 1)] = (pbuf[k, at(left, 1)] + far_l[k].astype(F32)).astype(BF16)
+        sbuf[k, at(left, 1), lanes] = (pbuf[k, at(left, 1), lanes] + far_l[k, :, lanes].astype(F32)).astype(BF16)
         onward[1].start()
 
-    def third(k):
-        for copy in near(k):
+    def third(unit):
+        k, s, lanes = unit
+        for copy in near(unit):
             copy.wait_recv()
-        return pbuf[k, at(c)] + near_r[k].astype(F32) + near_l[k].astype(F32)
-
-    def drain(k):
-        for copy in far(k) + near(k):
+        return pbuf[k, at(c), lanes] + near_r[k, :, lanes].astype(F32) + near_l[k, :, lanes].astype(F32)
+
+    def drain(unit):
+        for copy in far(unit) + near(unit):
             copy.wait_send()
 
     return first, second, third, drain
@@ -114,13 +120,14 @@
                  out_ref, wx_all, wy_all, wo_all, wg_all, wu_all, wd_all,
                  xbuf, pbufs, pv_ref, pos_ref, wide_ref, xown, pars, nall, mall, wtile, ctile, stage_r, stage_c, ubuf, hsend, hrecv, ybuf, abuf, bbuf, tot, mixed, gbuf, inner, res,
                  pbuf, sbuf, far_r, far_l, near_r, near_l, osend, fin,
-                 lsem, tsem, csem, outsem, xs, xr, ps, pr, ns, nr, hs, hr, ts, tr, as_, ar, ms, mr, ds, dr, os_, or_, fs, fr, ss, rs):
+                 lsem, tsem, csem, outsem, xs, xr, ps, pr, ns, nr, hs, hr, ts, tr, as_, ar, ms, mr, ds, dr, os_, or_, fs, fr, ss, rs, ws, wr):
     w, c = lax.axis_index('wd'), lax.axis_index('ch')
     nx = nw // 2
     chip, core = w // 2, w % 2
     rows, part = xown.shape[0], xbuf.shape[2]
     tokens, chans = ybuf.shape
     width = part * nw
+    slims = part // SLIM
 
     def member(step, other):
         return shifted(chip, step, nx) * 2 + (core + other) % 2
@@ -168,10 +175,15 @@
         def keep():
             return pltpu.make_async_copy(stage, mine, lsem.at[1])
 
-        return copy, load, keep
+        def slim(kind, t):
+            block, p, to = relays[(0, 1, 6, 7)[kind]]
+            rows_of_piece = piece(block, p).at[:, aligned(t * SLIM, SLIM)]
+            return remote(rows_of_piece, rows_of_piece, ws.at[kind, t], wr.at[kind, t], wd=to)
+
+        return copy, load, keep, slim
 
     def send_own(i):
-        copy, load, keep = stream(i)
+        copy, load, keep, slim = stream(i)
         for k in range(5):
             copy(k).start()
         load().start()
@@ -179,14 +191,17 @@
         keep().start()
 
     def send_on(i):
-        copy, load, keep = stream(i)
+        copy, load, keep, slim = stream(i)
         keep().wait()
-        copy(0).wait_recv()
-        copy(5).start()
-        copy(7).start()
-        copy(1).wait_recv()
-        copy(6).start()
-        copy(8).start()
+        last = i + 1 == len(weights)
+        for k in range(2):
+            copy(k).wait_recv()
+            if last:
+                for t in range(slims - 1):
+                    slim(k, t).start()
+            else:
+                copy(5 + k).start()
+            copy(7 + k).start()
 
     def send_on_and_next(i):
         send_on(i)
@@ -359,6 +374,9 @@
     ready(2)
     first, second, third, drain = ring_sums(c, nc, rows, pbuf, sbuf, far_r, far_l, near_r, near_l, as_, ar)
 
+    def whole(k):
+        return k, k, pl.ds(0, part)
+
     def o_load(j, slot):
         return pltpu.make_async_copy(wo_all.at[aligned(j * chans, chans)], ctile.at[slot, pl.ds(0, chans)], csem.at[slot])
 
@@ -372,11 +390,11 @@
             o_load(k + 1, 1 - slot).start()
 
         o_load(k, slot).wait()
-        first(k, jnp.dot(mixed[...], ctile[slot, pl.ds(0, chans), :], preferred_element_type=F32))
+        first(whole(k), jnp.dot(mixed[...], ctile[slot, pl.ds(0, chans), :], preferred_element_type=F32))
         return carry
 
     def o_second(k, carry):
-        second(k)
+        second(whole(k))
         return carry
 
     lax.fori_loop(0, nw, o_step, 0)
@@ -385,7 +403,7 @@
     total = jnp.zeros((rows, 1), F32)
     for k in range(nw):
         cols = slice(k * part, (k + 1) * part)
-        vals = xown[:, cols].astype(F32) + third(k) + pars[1:2, cols]
+        vals = xown[:, cols].astype(F32) + third(whole(k)) + pars[1:2, cols]
         res[:, cols] = vals
         total = total + jnp.sum(vals * vals, axis=1, keepdims=True)
     for k in range(nw):
@@ -395,7 +413,7 @@
     begin()
 
     def o_drain(k, carry):
-        drain(k)
+        drain(whole(k))
         return carry
 
     lax.fori_loop(0, nw, o_drain, 0)
@@ -439,10 +457,10 @@
     def source_of(d):
         return pick(d, sources)
 
-    down = stream(5)[0]
+    down, _, _, slim = stream(5)
 
     def arrived(d):
-        needs = {1: ((4, None),), 2: ((2, 9), (3, 10)), 4: ((7, None), (9, None)), 5: ((8, None), (10, None)), 6: ((5, 11), (6, 12)), 7: ((11, None), (12, None))}
+        needs = {1: ((4, None),), 2: ((2, 9), (3, 10)), 4: ((7, None), (9, None)), 5: ((8, None), (10, None))}
         for k, items in needs.items():
             @pl.when(d == k)
             def _():
@@ -454,115 +472,166 @@
     def rows_at(owner, group, at=0, size=rows):
         return aligned((owner * nc + group) * rows + at, size)
 
-    def hop(d):
-        return remote(osend.at[d], fin.at[rows_at(w, c)], os_.at[d], or_.at[d], wd=block_of(d))
-
-    def spread(d):
-        piece = fin.at[rows_at(source_of(d), c)]
-        return (remote(piece, piece, fs.at[0, d], fr.at[0, d], ch=right), remote(piece, piece, fs.at[1, d], fr.at[1, d], ch=left))
-
-    def relay(d):
-        from_left = fin.at[rows_at(source_of(d), left, 0, half)]
-        from_right = fin.at[rows_at(source_of(d), right, half, half)]
-        return (remote(from_left, from_left, fs.at[2, d], fr.at[2, d], ch=right), remote(from_right, from_right, fs.at[3, d], fr.at[3, d], ch=left))
-
-    def finish(e):
-        cols = aligned(block_of(e) * part, part)
-        done = (res[:, cols] + third(e) + pars[3:4, cols]).astype(BF16)
+    def hop(unit):
+        d, s, lanes = unit
+        return remote(osend.at[d, :, lanes], fin.at[rows_at(w, c), lanes], os_.at[s], or_.at[s], wd=block_of(d))
+
+    def spread(unit):
+        d, s, lanes = unit
+        piece = fin.at[rows_at(source_of(d), c), lanes]
+        return (remote(piece, piece, fs.at[0, s], fr.at[0, s], ch=right), remote(piece, piece, fs.at[1, s], fr.at[1, s], ch=left))
+
+    def relay(unit):
+        d, s, lanes = unit
+        from_left = fin.at[rows_at(source_of(d), left, 0, half), lanes]
+        from_right = fin.at[rows_at(source_of(d), right, half, half), lanes]
+        return (remote(from_left, from_left, fs.at[2, s], fr.at[2, s], ch=right), remote(from_right, from_right, fs.at[3, s], fr.at[3, s], ch=left))
+
+    def multiply(unit):
+        d, s, lanes = unit
+        target = ctile.at[0, :, lanes]
+        load = pltpu.make_async_copy(wd_all.at[aligned(block_of(d) * depth, depth), lanes], target, csem.at[0])
+        load.start()
+        load.wait()
+        first(unit, jnp.dot(inner[...], target[...], preferred_element_type=F32))
+
+    def finish(unit):
+        e, s, lanes = unit
+        cols = pl.ds(pl.multiple_of(block_of(e) * part + lanes.start, SLIM), lanes.size)
+        done = (res[:, cols] + third(unit) + pars[3:4, cols]).astype(BF16)
 
         @pl.when(e == 0)
         def _():
-            fin[rows_at(w, c), :] = done
+            fin[rows_at(w, c), lanes] = done
 
         @pl.when(e > 0)
         def _():
-            osend[e] = done
-            hop(e).start()
-
-    def share(e):
-        @pl.when(e > 0)
+            osend[e, :, lanes] = done
+            hop(unit).start()
+
+    def share(unit):
+        @pl.when(unit[0] > 0)
         def _():
-            hop(e).wait_recv()
-
-        for copy in spread(e):
+            hop(unit).wait_recv()
+
+        for copy in spread(unit):
             copy.start()
 
-    def pass_on(e):
-        for copy, onward in zip(spread(e), relay(e)):
+    def pass_on(unit):
+        for copy, onward in zip(spread(unit), relay(unit)):
             copy.wait_recv()
             onward.start()
 
-    def store(e):
+    def store(unit):
+        e, s, lanes = unit
         at = aligned(source_of(e) * tokens, tokens)
-        return pltpu.make_async_copy(fin.at[at], out_ref.at[at], outsem.at[e])
-
-    def complete(e):
-        for copy in relay(e):
+        return pltpu.make_async_copy(fin.at[at, lanes], out_ref.at[at, lanes], outsem.at[s])
+
+    def complete(unit):
+        for copy in relay(unit):
             copy.wait_recv()
-        store(e).start()
+        store(unit).start()
+
+    def settle(unit):
+        for copy in spread(unit) + relay(unit):
+            copy.wait_send()
+        drain(unit)
+
+        @pl.when(unit[0] > 0)
+        def _():
+            hop(unit).wait_send()
+
+        store(unit).wait()
+
+    def each(first_one, last_one, body):
+        def step(e, carry):
+            body(whole(e))
+            return carry
+
+        lax.fori_loop(first_one, last_one, step, 0)
+
+    fulls = nw - 2
+
+    def slim_units(t):
+        return [(fulls + k, fulls + 2 * t + k, pl.ds(t * SLIM, SLIM)) for k in range(2)]
 
     def d_step(d, carry):
         arrived(d)
-        load = pltpu.make_async_copy(wd_all.at[aligned(block_of(d) * depth, depth)], ctile.at[0], csem.at[0])
-        load.start()
-        load.wait()
-        first(d, jnp.dot(inner[...], ctile[0], preferred_element_type=F32))
+        multiply(whole(d))
 
         @pl.when(d >= 1)
         def _():
-            second(d - 1)
+            second(whole(d - 1))
 
         @pl.when(d >= 2)
         def _():
-            finish(d - 2)
+            finish(whole(d - 2))
 
         for k in (0, 1):
             @pl.when(d == k + 4)
             def _():
-                share(k)
-
-            @pl.when(d == k + 6)
-            def _():
-                pass_on(k)
+                share(whole(k))
 
         return carry
 
-    def each(first_one, last_one, body):
-        def step(e, carry):
-            body(e)
-            return carry
-
-        lax.fori_loop(first_one, last_one, step, 0)
-
-    lax.fori_loop(0, nw, d_step, 0)
-    second(nw - 1)
-    finish(nw - 2)
+    lax.fori_loop(0, fulls, d_step, 0)
+    for k in range(2):
+        slim(k, slims - 1).start()
+
+    def slim_step(t):
+        for k in range(2):
+            slim(k, t).wait_recv()
+            slim(2 + k, t).start()
+        same, other = slim_units(t)
+        multiply(same)
+        for k in range(2):
+            slim(2 + k, t).wait_recv()
+        multiply(other)
+
+    def do(body, t):
+        for unit in slim_units(t):
+            body(unit)
+
+    slim_step(0)
+    second(whole(fulls - 1))
+    finish(whole(fulls - 2))
+    each(0, 2, pass_on)
+    for t in range(1, slims):
+        slim_step(t)
+        do(second, t - 1)
+        if t == 1:
+            finish(whole(fulls - 1))
+        else:
+            do(finish, t - 2)
+    do(second, slims - 1)
     each(2, 4, share)
-    finish(nw - 1)
+    do(finish, slims - 2)
     each(4, 6, share)
     each(2, 4, pass_on)
-    share(6)
+    do(finish, slims - 1)
+    do(share, 0)
     each(4, 6, pass_on)
-    share(7)
-    each(6, 8, pass_on)
-    each(0, nw, complete)
-
-    def settle(d):
-        for copy in spread(d) + relay(d):
-            copy.wait_send()
-        drain(d)
-
-        @pl.when(d > 0)
-        def _():
-            hop(d).wait_send()
-
-    each(0, nw, settle)
+    for t in range(1, slims):
+        do(share, t)
+        do(pass_on, t - 1)
+    each(0, fulls, complete)
+    for t in range(slims - 1):
+        do(complete, t)
+    do(pass_on, slims - 1)
+    do(complete, slims - 1)
+    each(0, fulls, settle)
+    for t in range(slims):
+        do(settle, t)
     for i in range(len(weights)):
-        copy = stream(i)[0]
+        copy, _, _, slim = stream(i)
+        last = i + 1 == len(weights)
         for k in range(13):
-            copy(k).wait_send()
-    for k in range(nw):
-        store(k).wait()
+            if not (last and k in (5, 6, 11, 12)):
+                copy(k).wait_send()
+        if last:
+            for kind in range(4):
+                for t in range(slims):
+                    slim(kind, t).wait_send()
 
 
 def dma(*shape):
@@ -591,6 +660,8 @@
         def landing(arr):
             return jax.ShapeDtypeStruct((arr.shape[0] * nw, arr.shape[1]), arr.dtype)
 
+        slims = part // SLIM
+        units = nw - 2 + 2 * slims
         stream = (w_x, w_y, w_o, w_g, w_u, w_d)
         scratch = [
             VMEM((nw, rows, part), BF16), VMEM((nw, 8, part), F32), VMEM((16, chans), F32), VMEM((span, bw), jnp.int32), VMEM((8, wide), F32), VMEM((rows, width), BF16), VMEM((8, width), F32),
@@ -601,9 +672,9 @@
             VMEM((span, wide), F32), VMEM((span, wide), BF16), VMEM((rows, width), F32),
             VMEM((nw, span, part), F32), VMEM((nw, span, part), BF16), VMEM((nw, rows // 2, part), BF16), VMEM((nw, rows // 2, part), BF16),
             VMEM((nw, rows, part), BF16), VMEM((nw, rows, part), BF16), VMEM((nw, rows, part), BF16), VMEM((tokens, part), BF16),
-            dma(4), dma(2), dma(2), dma(nw), dma(nw), dma(nw), dma(nw), dma(nw), dma(6), dma(6), dma(1), dma(1), dma(nw), dma(nw),
-            dma(4, nw), dma(4, nw), dma(6), dma(6), dma(4, nw), dma(4, nw), dma(nw), dma(nw), dma(4, nw), dma(4, nw),
-            dma(len(stream), 13), dma(len(stream), 13),
+            dma(4), dma(2), dma(2), dma(units), dma(nw), dma(nw), dma(nw), dma(nw), dma(6), dma(6), dma(1), dma(1), dma(nw), dma(nw),
+            dma(4, nw), dma(4, nw), dma(6), dma(6), dma(4, units), dma(4, units), dma(units), dma(units), dma(4, units), dma(4, units),
+            dma(len(stream), 13), dma(len(stream), 13), dma(4, slims), dma(4, slims),
         ]
         return pl.pallas_call(
             functools.partial(layer_kernel, nw, nc), name='layer',

time: 314 us -> 323 us (1.029)
  Pallas kernels: 309 us -> 315 us
    pallas_call x1, Pallas kernels: 309 us -> 315 us  [local_layer(): pl.pallas_call(functools.partial(layer_kernel, nw, nc), name='layer', out...]
where the time goes in v2:
time: 323 us; the launch traced here: 319 us
  Pallas kernels  315 us (98%)
  local copies, waits for them, and re-layouts  3.87 us (1%)
    pallas_call x1, Pallas kernels, local_layer(): pl.pallas_call(functools.partial(layer_kernel, nw, nc), name='layer', out...  315 us

profile of v2, /device:TPU:97, one launch (start us, length us, event | category | flops | bytes accessed | tf_op | source)
XLA Modules:
  0.0 319.3 jit_solution(6938349603439318747)
XLA Ops:
  0.0 315.4 %layer.1 = (bf16[4096,384]{1,0:T(8,128)(2,1)}, bf16[3072,1024]{1,0:T(8,128)(2,1)}, bf16[3072,1024]{1,0:T(8,128)(2,1)}, bf16[8192,384]{1,0:T(8,128)(2,1)}, bf16[3...) custom-call(bf16[4096,384]{1,0:T(8,128)(2,1)} %x_ref.1, s32[1,4096]{1,0:T(1,128)} %seg_ref.1, ...), custom_call_target="tpu_custom_call" | custom-call | tf_op jit(solution)/shard_map/layer/pallas_call | solution.py:679
  315.4 3.9 %copy.25 = bf16[4096,384]{1,0:T(8,128)(2,1)} copy(bf16[4096,384]{1,0:T(8,128)(2,1)} %get-tuple-element.6) | data formatting | bytes 6291456

commit v3 on v1

--- a/solution.py
+++ b/solution.py
@@ -8,6 +8,7 @@
 from jax.sharding import PartitionSpec as P
 
 EPS = 1e-6
+PIECES = 3
 F32 = jnp.float32
 BF16 = jnp.bfloat16
 MESH = pl.DeviceIdType.MESH
@@ -114,7 +115,7 @@
                  out_ref, wx_all, wy_all, wo_all, wg_all, wu_all, wd_all,
                  xbuf, pbufs, pv_ref, pos_ref, wide_ref, xown, pars, nall, mall, wtile, ctile, stage_r, stage_c, ubuf, hsend, hrecv, ybuf, abuf, bbuf, tot, mixed, gbuf, inner, res,
                  pbuf, sbuf, far_r, far_l, near_r, near_l, osend, fin,
-                 lsem, tsem, csem, outsem, xs, xr, ps, pr, ns, nr, hs, hr, ts, tr, as_, ar, ms, mr, ds, dr, os_, or_, fs, fr, ss, rs):
+                 lsem, tsem, csem, outsem, xs, xr, ps, pr, ns, nr, hs, hr, ts, tr, as_, ar, ms, mr, ds, dr, os_, or_, fs, fr, ss, rs, ws, wr):
     w, c = lax.axis_index('wd'), lax.axis_index('ch')
     nx = nw // 2
     chip, core = w // 2, w % 2
@@ -168,10 +169,16 @@
         def keep():
             return pltpu.make_async_copy(stage, mine, lsem.at[1])
 
-        return copy, load, keep
+        def part_copy(kind, t):
+            block, p, to = relays[(0, 1, 6, 7)[kind]]
+            size = half // PIECES
+            rows_of_piece = dst.at[aligned(block * depth + p * half + t * size, size)]
+            return remote(rows_of_piece, rows_of_piece, ws.at[kind, t], wr.at[kind, t], wd=to)
+
+        return copy, load, keep, part_copy
 
     def send_own(i):
-        copy, load, keep = stream(i)
+        copy, load, keep, part_copy = stream(i)
         for k in range(5):
             copy(k).start()
         load().start()
@@ -179,14 +186,18 @@
         keep().start()
 
     def send_on(i):
-        copy, load, keep = stream(i)
-        keep().wait()
-        copy(0).wait_recv()
-        copy(5).start()
-        copy(7).start()
-        copy(1).wait_recv()
-        copy(6).start()
-        copy(8).start()
+        copy, load, keep, part_copy = stream(i)
+        last = i + 1 == len(weights)
+        if not last:
+            keep().wait()
+        for k in range(2):
+            copy(k).wait_recv()
+            if last:
+                for t in range(PIECES - 1):
+                    part_copy(k, t).start()
+            else:
+                copy(5 + k).start()
+            copy(7 + k).start()
 
     def send_on_and_next(i):
         send_on(i)
@@ -417,39 +428,22 @@
         inner[:, cols] = (gbuf[:, cols] * u).astype(BF16)
 
     column_tiles(wu_all, i_tile)
-    send_on(5)
 
     first, second, third, drain = ring_sums(c, nc, rows, pbuf, sbuf, far_r, far_l, near_r, near_l, ds, dr)
     right, left = shifted(c, 1, nc), shifted(c, -1, nc)
     half = rows // 2
     depth = wd.shape[0]
 
-    def pick(d, options):
-        value = options[0]
-        for k in range(1, nw):
-            value = jnp.where(d == k, options[k], value)
-        return value
-
     targets = [member(step, other) for step, other in HOPS]
     sources = [member(-step, other) for step, other in HOPS]
 
     def block_of(d):
-        return pick(d, targets)
+        return targets[d]
 
     def source_of(d):
-        return pick(d, sources)
-
-    down = stream(5)[0]
-
-    def arrived(d):
-        needs = {1: ((4, None),), 2: ((2, 9), (3, 10)), 4: ((7, None), (9, None)), 5: ((8, None), (10, None)), 6: ((5, 11), (6, 12)), 7: ((11, None), (12, None))}
-        for k, items in needs.items():
-            @pl.when(d == k)
-            def _():
-                for index, onward in items:
-                    down(index).wait_recv()
-                    if onward is not None:
-                        down(onward).start()
+        return sources[d]
+
+    down, _, keep, part_copy = stream(5)
 
     def rows_at(owner, group, at=0, size=rows):
         return aligned((owner * nc + group) * rows + at, size)
@@ -470,20 +464,15 @@
         cols = aligned(block_of(e) * part, part)
         done = (res[:, cols] + third(e) + pars[3:4, cols]).astype(BF16)
 
-        @pl.when(e == 0)
-        def _():
+        if e == 0:
             fin[rows_at(w, c), :] = done
-
-        @pl.when(e > 0)
-        def _():
+        else:
             osend[e] = done
             hop(e).start()
 
     def share(e):
-        @pl.when(e > 0)
-        def _():
+        if e > 0:
             hop(e).wait_recv()
-
         for copy in spread(e):
             copy.start()
 
@@ -501,66 +490,106 @@
             copy.wait_recv()
         store(e).start()
 
-    def d_step(d, carry):
-        arrived(d)
-        load = pltpu.make_async_copy(wd_all.at[aligned(block_of(d) * depth, depth)], ctile.at[0], csem.at[0])
-        load.start()
-        load.wait()
-        first(d, jnp.dot(inner[...], ctile[0], preferred_element_type=F32))
-
-        @pl.when(d >= 1)
-        def _():
-            second(d - 1)
-
-        @pl.when(d >= 2)
-        def _():
-            finish(d - 2)
-
-        for k in (0, 1):
-            @pl.when(d == k + 4)
-            def _():
-                share(k)
-
-            @pl.when(d == k + 6)
-            def _():
-                pass_on(k)
-
-        return carry
-
-    def each(first_one, last_one, body):
-        def step(e, carry):
-            body(e)
-            return carry
-
-        lax.fori_loop(first_one, last_one, step, 0)
-
-    lax.fori_loop(0, nw, d_step, 0)
-    second(nw - 1)
-    finish(nw - 2)
-    each(2, 4, share)
-    finish(nw - 1)
-    each(4, 6, share)
-    each(2, 4, pass_on)
+    def fetch(d):
+        return pltpu.make_async_copy(wd_all.at[aligned(block_of(d) * depth, depth)], ctile.at[d % 2], csem.at[d % 2])
+
+    def multiply(d):
+        fetch(d).wait()
+        first(d, jnp.dot(inner[...], ctile[d % 2], preferred_element_type=F32))
+
+    def take(*indices):
+        for k in indices:
+            down(k).wait_recv()
+
+    def relay_piece(t):
+        for k in range(2):
+            part_copy(k, t).wait_recv()
+            part_copy(2 + k, t).start()
+
+    keep().wait()
+    fetch(0).start()
+    take(4)
+    fetch(1).start()
+    multiply(0)
+    multiply(1)
+    send_on(5)
+    second(0)
+    second(1)
+    finish(0)
+    share(0)
+    finish(1)
+    share(1)
+    pass_on(0)
+    pass_on(1)
+    take(2, 3)
+    fetch(2).start()
+    fetch(3).start()
+    down(9).start()
+    down(10).start()
+    multiply(2)
+    take(7, 9)
+    fetch(4).start()
+    multiply(3)
+    second(2)
+    take(8, 10)
+    fetch(5).start()
+    multiply(4)
+    second(3)
+    finish(2)
+    multiply(5)
+    finish(3)
+    for k in range(2):
+        part_copy(k, PIECES - 1).start()
+    second(4)
+    for t in range(PIECES - 1):
+        relay_piece(t)
+    finish(4)
+    second(5)
+    finish(5)
+    share(2)
+    share(3)
+    relay_piece(PIECES - 1)
+    fetch(6).start()
+    pass_on(2)
+    pass_on(3)
+    multiply(6)
+    for t in range(PIECES):
+        for k in range(2):
+            part_copy(2 + k, t).wait_recv()
+    fetch(7).start()
+    share(4)
+    share(5)
+    multiply(7)
+    second(6)
+    pass_on(4)
+    pass_on(5)
+    second(7)
+    finish(6)
+    finish(7)
     share(6)
-    each(4, 6, pass_on)
     share(7)
-    each(6, 8, pass_on)
-    each(0, nw, complete)
-
-    def settle(d):
-        for copy in spread(d) + relay(d):
+    for e in range(6):
+        complete(e)
+    pass_on(6)
+    pass_on(7)
+    complete(6)
+    complete(7)
+    for e in range(nw):
+        for copy in spread(e) + relay(e):
             copy.wait_send()
-        drain(d)
-
-        @pl.when(d > 0)
-        def _():
-            hop(d).wait_send()
-
-    each(0, nw, settle)
+        drain(e)
+        if e > 0:
+            hop(e).wait_send()
     for i in range(len(weights)):
-        copy = stream(i)[0]
+        copy, _, _, part_copy = stream(i)
+        last = i + 1 == len(weights)
         for k in range(13):
-            copy(k).wait_send()
+            if not (last and k in (5, 6, 11, 12)):
+                copy(k).wait_send()
+        if last:
+            for kind in range(4):
+                for t in range(PIECES):
+                    part_copy(kind, t).wait_send()
     for k in range(nw):
         store(k).wait()
 
@@ -603,7 +632,7 @@
             VMEM((nw, rows, part), BF16), VMEM((nw, rows, part), BF16), VMEM((nw, rows, part), BF16), VMEM((tokens, part), BF16),
             dma(4), dma(2), dma(2), dma(nw), dma(nw), dma(nw), dma(nw), dma(nw), dma(6), dma(6), dma(1), dma(1), dma(nw), dma(nw),
             dma(4, nw), dma(4, nw), dma(6), dma(6), dma(4, nw), dma(4, nw), dma(nw), dma(nw), dma(4, nw), dma(4, nw),
-            dma(len(stream), 13), dma(len(stream), 13),
+            dma(len(stream), 13), dma(len(stream), 13), dma(4, PIECES), dma(4, PIECES),
         ]
         return pl.pallas_call(
             functools.partial(layer_kernel, nw, nc), name='layer',

time: 314 us -> 315 us (level)
  no operation moved by 1% of the time
where the time goes in v3:
time: 315 us; the launch traced here: 314 us
  Pallas kernels  310 us (98%)
  local copies, waits for them, and re-layouts  3.87 us (1%)
    pallas_call x1, Pallas kernels, local_layer(): pl.pallas_call(functools.partial(layer_kernel, nw, nc), name='layer', out...  310 us

profile of v3, /device:TPU:97, one launch (start us, length us, event | category | flops | bytes accessed | tf_op | source)
XLA Modules:
  0.0 314.2 jit_solution(2087147495489078700)
XLA Ops:
  0.0 310.3 %layer.1 = (bf16[4096,384]{1,0:T(8,128)(2,1)}, bf16[3072,1024]{1,0:T(8,128)(2,1)}, bf16[3072,1024]{1,0:T(8,128)(2,1)}, bf16[8192,384]{1,0:T(8,128)(2,1)}, bf16[3...) custom-call(bf16[4096,384]{1,0:T(8,128)(2,1)} %x_ref.1, s32[1,4096]{1,0:T(1,128)} %seg_ref.1, ...), custom_call_target="tpu_custom_call" | custom-call | tf_op jit(solution)/shard_map/layer/pallas_call | solution.py:637
  310.3 3.9 %copy.25 = bf16[4096,384]{1,0:T(8,128)(2,1)} copy(bf16[4096,384]{1,0:T(8,128)(2,1)} %get-tuple-element.6) | data formatting | bytes 6291456

commit v4 on v3

--- a/solution.py
+++ b/solution.py
@@ -543,34 +543,36 @@
     second(4)
     for t in range(PIECES - 1):
         relay_piece(t)
+    second(5)
+    share(2)
     finish(4)
-    second(5)
+    share(3)
     finish(5)
-    share(2)
-    share(3)
     relay_piece(PIECES - 1)
     fetch(6).start()
     pass_on(2)
-    pass_on(3)
     multiply(6)
     for t in range(PIECES):
         for k in range(2):
             part_copy(2 + k, t).wait_recv()
     fetch(7).start()
     share(4)
+    multiply(7)
+    pass_on(3)
+    second(6)
     share(5)
-    multiply(7)
-    second(6)
+    second(7)
     pass_on(4)
+    finish(6)
     pass_on(5)
-    second(7)
-    finish(6)
     finish(7)
     share(6)
+    for e in range(4):
+        complete(e)
     share(7)
-    for e in range(6):
-        complete(e)
     pass_on(6)
+    complete(4)
+    complete(5)
     pass_on(7)
     complete(6)
     complete(7)

time: 315 us -> 312 us (level)
    pallas_call x1, Pallas kernels: 310 us -> 307 us  [local_layer(): pl.pallas_call(functools.partial(layer_kernel, nw, nc), name='layer', out...]
where the time goes in v4:
time: 312 us; the launch traced here: 311 us
  Pallas kernels  307 us (98%)
  local copies, waits for them, and re-layouts  3.87 us (1%)
    pallas_call x1, Pallas kernels, local_layer(): pl.pallas_call(functools.partial(layer_kernel, nw, nc), name='layer', out...  307 us

profile of v4, /device:TPU:97, one launch (start us, length us, event | category | flops | bytes accessed | tf_op | source)
XLA Modules:
  0.0 310.8 jit_solution(1105785872375139818)
XLA Ops:
  0.0 307.0 %layer.1 = (bf16[4096,384]{1,0:T(8,128)(2,1)}, bf16[3072,1024]{1,0:T(8,128)(2,1)}, bf16[3072,1024]{1,0:T(8,128)(2,1)}, bf16[8192,384]{1,0:T(8,128)(2,1)}, bf16[3...) custom-call(bf16[4096,384]{1,0:T(8,128)(2,1)} %x_ref.1, s32[1,4096]{1,0:T(1,128)} %seg_ref.1, ...), custom_call_target="tpu_custom_call" | custom-call | tf_op jit(solution)/shard_map/layer/pallas_call | solution.py:639
  307.0 3.9 %copy.25 = bf16[4096,384]{1,0:T(8,128)(2,1)} copy(bf16[4096,384]{1,0:T(8,128)(2,1)} %get-tuple-element.6) | data formatting | bytes 6291456

commit v5 on v4

--- a/solution.py
+++ b/solution.py
@@ -17,7 +17,6 @@
 HALO = 16
 TILE = 8
 VMEM_LIMIT = 62 * 1024 * 1024
-HOPS = ((0, 0), (0, 1), (-1, 0), (1, 0), (-1, 1), (1, 1), (2, 0), (2, 1))
 
 
 def remote(src, dst, send, recv, **to):
@@ -126,6 +125,12 @@
     def member(step, other):
         return shifted(chip, step, nx) * 2 + (core + other) % 2
 
+    lead = jnp.where(core == 0, 1, nx - 1)
+
+    def beside(step, other):
+        return lax.rem(chip + step, nx) * 2 + (core + other) % 2
+
+    fore_w, back_w = beside(lead, 0), beside(nx - lead, 0)
     right_w, left_w, far_w, mate = member(1, 0), member(-1, 0), member(2, 0), member(0, 1)
 
     barrier = pltpu.get_barrier_semaphore()
@@ -147,8 +152,13 @@
 
         low, high = src.at[pl.ds(0, half)], src.at[pl.ds(half, half)]
         mine = dst.at[aligned(w * depth, depth)]
-        first_sends = ((low, piece(w, 0), right_w), (high, piece(w, 1), left_w), (high, piece(w, 1), right_w), (low, piece(w, 0), left_w), (src, mine, mate))
-        relays = ((left_w, 0, right_w), (right_w, 1, left_w), (left_w, 0, mate), (right_w, 1, mate), (left_w, 1, mate), (right_w, 0, mate), (far_w, 0, mate), (far_w, 1, mate))
+        last = i + 1 == len(weights)
+        if last:
+            first_sends = ((low, piece(w, 0), fore_w), (high, piece(w, 1), fore_w), (high, piece(w, 1), back_w), (low, piece(w, 0), back_w), (src, mine, mate))
+            relays = ((back_w, 0, fore_w), (fore_w, 1, back_w), (back_w, 0, mate), (back_w, 1, mate), (fore_w, 1, mate), (fore_w, 0, mate), (far_w, 0, mate), (far_w, 1, mate))
+        else:
+            first_sends = ((low, piece(w, 0), right_w), (high, piece(w, 1), left_w), (high, piece(w, 1), right_w), (low, piece(w, 0), left_w), (src, mine, mate))
+            relays = ((left_w, 0, right_w), (right_w, 1, left_w), (left_w, 0, mate), (right_w, 1, mate), (left_w, 1, mate), (right_w, 0, mate), (far_w, 0, mate), (far_w, 1, mate))
 
         def copy(k):
             if k < len(first_sends):
@@ -180,23 +190,18 @@
     def send_own(i):
         copy, load, keep, part_copy = stream(i)
         for k in range(5):
-            copy(k).start()
+            if i + 1 < len(weights) or k not in (2, 3):
+                copy(k).start()
         load().start()
         load().wait()
         keep().start()
 
     def send_on(i):
         copy, load, keep, part_copy = stream(i)
-        last = i + 1 == len(weights)
-        if not last:
-            keep().wait()
+        keep().wait()
         for k in range(2):
             copy(k).wait_recv()
-            if last:
-                for t in range(PIECES - 1):
-                    part_copy(k, t).start()
-            else:
-                copy(5 + k).start()
+            copy(5 + k).start()
             copy(7 + k).start()
 
     def send_on_and_next(i):
@@ -434,8 +439,8 @@
     half = rows // 2
     depth = wd.shape[0]
 
-    targets = [member(step, other) for step, other in HOPS]
-    sources = [member(-step, other) for step, other in HOPS]
+    targets = [w, mate, back_w, beside(lead, 1), fore_w, beside(nx - lead, 1), far_w, member(2, 1)]
+    sources = [w, mate, fore_w, beside(lead, 1), back_w, beside(nx - lead, 1), far_w, member(2, 1)]
 
     def block_of(d):
         return targets[d]
@@ -512,41 +517,49 @@
     fetch(1).start()
     multiply(0)
     multiply(1)
-    send_on(5)
+    down(2).start()
+    down(3).start()
+    take(0, 1)
+    fetch(2).start()
+    down(7).start()
+    down(8).start()
     second(0)
     second(1)
+    multiply(2)
     finish(0)
     share(0)
     finish(1)
+    take(7, 8)
+    fetch(3).start()
     share(1)
+    second(2)
+    multiply(3)
+    take(2)
+    down(9).start()
+    for t in range(PIECES - 1):
+        for k in range(2):
+            part_copy(k, t).start()
     pass_on(0)
     pass_on(1)
-    take(2, 3)
-    fetch(2).start()
-    fetch(3).start()
-    down(9).start()
+    finish(2)
+    second(3)
+    finish(3)
+    take(3)
+    fetch(4).start()
     down(10).start()
-    multiply(2)
-    take(7, 9)
-    fetch(4).start()
-    multiply(3)
-    second(2)
-    take(8, 10)
-    fetch(5).start()
     multiply(4)
-    second(3)
-    finish(2)
-    multiply(5)
-    finish(3)
     for k in range(2):
         part_copy(k, PIECES - 1).start()
+    take(9, 10)
+    fetch(5).start()
     second(4)
+    multiply(5)
+    share(2)
+    share(3)
+    finish(4)
+    second(5)
     for t in range(PIECES - 1):
         relay_piece(t)
-    second(5)
-    share(2)
-    finish(4)
-    share(3)
     finish(5)
     relay_piece(PIECES - 1)
     fetch(6).start()
@@ -603,7 +616,7 @@
 def solution(mesh):
     nw = mesh.shape['wd']
     nc = mesh.shape['ch']
-    assert nc == 4 and nw == len(HOPS)
+    assert nc == 4 and nw == 8
     row_spec = P('dp', 'wd')
     specs = (row_spec, P('dp', None), P('wd'), P('wd', 'ch'), P('ch'), P('wd', 'ch'), P('ch'), P(None, 'ch'), P('ch'), P('ch'), P('ch', None, None), P('ch'), P('ch', None, None), P('ch'), P('ch', 'wd'), P('wd'), P('wd'), P('wd', 'ch'), P('ch'), P('wd', 'ch'), P('ch'), P('ch', 'wd'), P('wd'))
     vm = pl.BlockSpec(memory_space=VMEM)

time: 312 us -> 318 us (1.019)
  Pallas kernels: 307 us -> 313 us
    pallas_call x1, Pallas kernels: 307 us -> 313 us  [local_layer(): pl.pallas_call(functools.partial(layer_kernel, nw, nc), name='layer', out...]
where the time goes in v5:
time: 318 us; the launch traced here: 317 us
  Pallas kernels  313 us (98%)
  local copies, waits for them, and re-layouts  3.87 us (1%)
    pallas_call x1, Pallas kernels, local_layer(): pl.pallas_call(functools.partial(layer_kernel, nw, nc), name='layer', out...  313 us

profile of v5, /device:TPU:97, one launch (start us, length us, event | category | flops | bytes accessed | tf_op | source)
XLA Modules:
  0.0 316.7 jit_solution(16113517389306108802)
XLA Ops:
  0.0 312.8 %layer.1 = (bf16[4096,384]{1,0:T(8,128)(2,1)}, bf16[3072,1024]{1,0:T(8,128)(2,1)}, bf16[3072,1024]{1,0:T(8,128)(2,1)}, bf16[8192,384]{1,0:T(8,128)(2,1)}, bf16[3...) custom-call(bf16[4096,384]{1,0:T(8,128)(2,1)} %x_ref.1, s32[1,4096]{1,0:T(1,128)} %seg_ref.1, ...), custom_call_target="tpu_custom_call" | custom-call | tf_op jit(solution)/shard_map/layer/pallas_call | solution.py:652
  312.8 3.9 %copy.25 = bf16[4096,384]{1,0:T(8,128)(2,1)} copy(bf16[4096,384]{1,0:T(8,128)(2,1)} %get-tuple-element.6) | data formatting | bytes 6291456
